TPU v7x, 256 devices: a whole 4x4x8 slice. The times are simulated.
256 devices in a mesh: grp: 2 (over core), blk: 128 (over y, z, x).
Axes of the slice: x: 4, y: 4, z: 8, core: 2. Of those that a mesh axis runs over, the one named last changes fastest.
Arguments:
- field: bfloat16 [256, 1048576], P('blk', 'grp'), may hold values from -4 to 4
- response: float32 [65], replicated, may hold values from 0.3 to 1
- area_weight: float32 [1048576], P(('grp', 'blk')), may hold values from 0.3 to 3
Outputs:
- patterns: float32 [256, 1048576], P(None, ('grp', 'blk'))
- scaled_r: float32 [256, 256], replicated
All inputs are finite; a program needn't handle non-finite values.
Results may differ from a plain program's by a relative error of at most 0.00055.
Values may be sent and summed in bfloat16 or wider, within the bound.
A program may use at most 128 MiB of HBM per device.

v0:
```python
import jax
import jax.numpy as jnp
from jax import lax
from jax.sharding import PartitionSpec as P

MONTHS = 128
MEMBERS = 2


TOP_PRECISION = lax.Precision.HIGHEST


def solve_lower(matrix, rhs):
    return lax.linalg.triangular_solve(matrix, rhs, left_side=True, lower=True)


def filter_matrix(response, months):
    bins = response.shape[0]
    freq = jnp.arange(bins, dtype=jnp.int32)
    edge = (freq == 0) | (freq == months // 2)
    coef = jnp.where(edge, 1.0, 2.0).astype(jnp.float32) * response / months
    times = jnp.arange(months, dtype=jnp.int32)
    offset = times[:, None] - times[None, :]
    phase = offset[:, :, None] * freq[None, None, :] % months
    table = jnp.cos(2.0 * jnp.pi * phase.astype(jnp.float32) / months)
    return jnp.einsum("tsk,k->ts", table, coef, precision=TOP_PRECISION)


def gram_of(column_row_pairs):
    return jnp.dot(
        column_row_pairs,
        column_row_pairs.T,
        precision=TOP_PRECISION,
        preferred_element_type=jnp.float32,
    )


def global_gram(matrix):
    return lax.psum(matrix, ("grp", "blk"))


def shards(field, response, area_weight):
    months = MONTHS
    members = MEMBERS
    regrouped = lax.all_to_all(field, "blk", split_axis=1, concat_axis=0, tiled=True)
    rows = regrouped.shape[1]
    mixing_weight = filter_matrix(response, months)
    time_series = regrouped.astype(jnp.float32).reshape(members, months, rows)
    lowpass_result = jnp.einsum("ab,ibg->iag", mixing_weight, time_series, precision=TOP_PRECISION)
    column_row_pairs = lowpass_result.reshape(members * months, rows) * area_weight[None, :]
    lower_one = jnp.linalg.cholesky(global_gram(gram_of(column_row_pairs)))
    basis = solve_lower(lower_one, column_row_pairs)
    lower_two = jnp.linalg.cholesky(global_gram(gram_of(basis)))
    upper_factor = jnp.dot(lower_one, lower_two, precision=TOP_PRECISION).T
    total_points = rows * lax.axis_size("grp") * lax.axis_size("blk")
    scale = jnp.sqrt(jnp.float32(total_points))
    q_rows = solve_lower(upper_factor.T, column_row_pairs)
    return (q_rows * scale, upper_factor / scale)


def solution(mesh):
    in_specs = (P("blk", "grp"), P(), P(("grp", "blk")))
    out_specs = (P(None, ("grp", "blk")), P())
    return jax.shard_map(shards, mesh=mesh, in_specs=in_specs, out_specs=out_specs, check_vma=False)
```

profile of v0, /device:TPU:1, one launch (start us, length us, event | category | flops | bytes accessed | tf_op | source)
XLA Modules:
  0.0 743.9 jit_solution(9613039994155191036)
XLA Ops:
  7.2 16.3 %all-to-all-start = ((bf16[2,128,4096]{2,0,1:T(2,128)(2,1)}), bf16[2,128,4096]{2,0,1:T(2,128)(2,1)S(1)}, u32[]{:S(2)}, u32[]{:S(2)}) async-start(bf16[2,128,4096]{2,0,1:T(2,128)(2,1)} %bitcast.84), calls=%async_computation | async-start | bytes 4194304 | tf_op jit(solution)/shard_map/all_to_all | solution.py:45
  23.6 15.4 %fusion.5 = f32[128,128,65]{1,0,2:T(8,128)S(1)} fusion(s32[128,128]{1,0:T(8,128)S(1)} %iota_subtract_fusion), kind=kLoop, calls=%fused_computation.14 | loop fusion | flops 14909440 | bytes 4325376 | tf_op jit(solution)/shard_map/cos | solution.py:25
  39.1 5.0 fusion
  44.1 28.8 %all-to-all-done = bf16[2,128,4096]{2,0,1:T(2,128)(2,1)S(1)} async-done(((bf16[2,128,4096]{2,0,1:T(2,128)(2,1)}), bf16[2,128,4096]{2,0,1:T(2,128)(2,1)S(1)}, u32[]{:S(2)}, u32[]{:S(2)}) %all-to-all-start) | async-done | bytes 2097184 | tf_op jit(solution)/shard_map/all_to_all | solution.py:45
  72.9 1.3 copy-done.2
  74.2 2.7 reshape.55
  76.9 3.8 bitcast_multiply_fusion.1
  80.8 4.2 fusion.64
  85.2 4.7 bitcast_multiply_fusion
  89.9 245.9 %all-reduce.4.cloned.1.call-done = f32[256,256]{0,1:T(8,128)} async-done(((f32[256,256]{0,1:T(8,128)}), f32[256,256]{0,1:T(8,128)}) %all-reduce.4.cloned.1.call-update) | async-done | bytes 262160 | tf_op jit(solution)/shard_map/psum | solution.py:39
  335.8 1.1 copy.13
  336.9 1.0 fusion.18
  337.9 11.7 %cholesky.130 = f32[128,128]{1,0:T(8,128)S(1)} custom-call(f32[128,128]{1,0:T(8,128)S(1)} %cholesky.194), custom_call_target="Cholesky" | custom-call | tf_op jit(solution)/shard_map/jit(cholesky)/cholesky | solution.py:51
  349.7 9.8 %custom-call.13 = f32[1,128,128]{1,2,0:T(8,128)S(1)} custom-call(f32[1,128,128]{2,1,0:T(8,128)S(1)} %get-tuple-element.53), custom_call_target="InvertDiagBlocksLowerTriangular" | custom-call | tf_op jit(solution)/shard_map/jit(cholesky)/cholesky | solution.py:51
  359.7 0.3 convolution_subtract_fusion.3
  360.0 11.7 %cholesky.147 = f32[128,128]{1,0:T(8,128)S(1)} custom-call(f32[128,128]{1,0:T(8,128)S(1)} %convolution_subtract_fusion.3), custom_call_target="Cholesky" | custom-call | tf_op jit(solution)/shard_map/jit(cholesky)/cholesky | solution.py:51
  371.7 0.6 compare_reduce_fusion.2
  373.8 4.0 while.4
  373.8 0.6 fusion.79
  374.4 1.4 bitcast_dynamic-update-slice_fusion.4
  375.8 0.6 fusion.79
  376.4 1.4 bitcast_dynamic-update-slice_fusion.4
  377.8 19.9 %custom-call.14 = f32[2,128,128]{1,2,0:T(8,128)S(1)} custom-call(f32[2,128,128]{2,1,0:T(8,128)S(1)} %get-tuple-element.18), custom_call_target="InvertDiagBlocksLowerTriangular" | custom-call | tf_op jit(solution)/shard_map/triangular_solve/custom-call.0 | solution.py:14
  397.7 3.6 fusion.15
  401.4 1.9 convolution_subtract_fusion.1
  403.3 1.9 fusion.36
  405.3 4.2 fusion.9
  409.5 253.2 %all-reduce.6.cloned.1.call-done = f32[256,256]{0,1:T(8,128)} async-done(((f32[256,256]{0,1:T(8,128)}), f32[256,256]{0,1:T(8,128)}) %all-reduce.6.cloned.1.call-update) | async-done | bytes 262160 | tf_op jit(solution)/shard_map/psum | solution.py:39
  662.8 1.1 copy.15
  663.8 1.0 fusion.17
  664.9 12.1 %cholesky.164 = f32[128,128]{1,0:T(8,128)S(1)} custom-call(f32[128,128]{1,0:T(8,128)S(1)} %cholesky.197), custom_call_target="Cholesky" | custom-call | tf_op jit(solution)/shard_map/jit(cholesky)/cholesky | solution.py:53
  677.0 9.8 %custom-call.15 = f32[1,128,128]{1,2,0:T(8,128)S(1)} custom-call(f32[1,128,128]{2,1,0:T(8,128)S(1)} %get-tuple-element.49), custom_call_target="InvertDiagBlocksLowerTriangular" | custom-call | tf_op jit(solution)/shard_map/jit(cholesky)/cholesky | solution.py:53
  687.0 0.3 convolution_subtract_fusion.2
  687.3 11.7 %cholesky.181 = f32[128,128]{1,0:T(8,128)S(1)} custom-call(f32[128,128]{1,0:T(8,128)S(1)} %convolution_subtract_fusion.2), custom_call_target="Cholesky" | custom-call | tf_op jit(solution)/shard_map/jit(cholesky)/cholesky | solution.py:53
  699.1 0.6 compare_reduce_fusion
  699.7 0.6 compare_reduce_fusion.1
  701.6 0.4 multiply_bitcast_fusion
  702.1 4.0 while.5
  702.1 0.6 fusion.80
  702.7 1.4 bitcast_dynamic-update-slice_fusion.5
  704.1 0.6 fusion.80
  704.7 1.4 bitcast_dynamic-update-slice_fusion.5
  706.1 19.8 %custom-call.16 = f32[2,128,128]{1,2,0:T(8,128)S(1)} custom-call(f32[2,128,128]{2,1,0:T(8,128)S(1)} %get-tuple-element.19), custom_call_target="InvertDiagBlocksLowerTriangular" | custom-call | tf_op jit(solution)/shard_map/triangular_solve/custom-call.0 | solution.py:14
  725.9 3.6 fusion.13
  729.6 1.9 convolution_subtract_fusion
  731.5 1.9 fusion.32
  733.5 2.5 maximum_multiply_fusion
  736.0 0.8 copy.16
  (33 shorter events, 1.1 us)
Async XLA Ops:
  7.2 31.9 %copy-start.4 = (f32[65]{0:T(128)S(1)}, f32[65]{0:T(128)}, u32[]{:S(2)}) copy-start(f32[65]{0:T(128)} %param.7) | copy-start | bytes 784
  7.2 65.7 %all-to-all-start = ((bf16[2,128,4096]{2,0,1:T(2,128)(2,1)}), bf16[2,128,4096]{2,0,1:T(2,128)(2,1)S(1)}, u32[]{:S(2)}, u32[]{:S(2)}) async-start(bf16[2,128,4096]{2,0,1:T(2,128)(2,1)} %bitcast.84), calls=%async_computation | async-start | bytes 4194304 | tf_op jit(solution)/shard_map/all_to_all | solution.py:45
  23.5 312.3 %all-reduce.4.cloned.1.call-start = ((), (), s32[]{:S(2)}) async-start(), calls=%async_computation.1 | async-start | bytes 524288 | tf_op jit(solution)/shard_map/psum | solution.py:39
  39.0 37.9 %copy-start.3 = (f32[4096]{0:T(1024)S(1)}, f32[4096]{0:T(1024)}, u32[]{:S(2)}) copy-start(f32[4096]{0:T(1024)} %param.8) | copy-start | bytes 49156
  72.9 1.3 copy-start.2
  85.0 577.8 %all-reduce.6.cloned.1.call-start = ((), (), s32[]{:S(2)}) async-start(), calls=%async_computation.2 | async-start | bytes 524288 | tf_op jit(solution)/shard_map/psum | solution.py:39
  397.7 3.7 copy-start
  725.9 3.7 copy-start.1
Sparse Core Ops, SparseCore 0:
  85.1 250.6 all-reduce.3
  409.6 253.0 all-reduce.5
where the time goes:
time: 755 us; the launch traced here: 744 us
  waiting for transfers between devices  528 us (70%)
  other arithmetic  133 us (18%)
  matrix products  33.7 us (4%)
  between operations  17.1 us (2%)
  starting transfers between devices  16.6 us (2%)
  local copies, waits for them, and re-layouts  15.1 us (2%)
    psum x2, waiting for transfers between devices, global_gram(): return lax.psum(matrix, ('grp', 'blk'))  499 us
    another operation x4, other arithmetic, solve_lower(): return lax.linalg.triangular_solve(matrix, rhs, left_side=True, lower=True)  39.8 us
    another operation x7, other arithmetic, shards(): lower_two = jnp.linalg.cholesky(global_gram(gram_of(basis)))  35 us
    another operation x6, other arithmetic, shards(): lower_one = jnp.linalg.cholesky(global_gram(gram_of(column_row_pairs)))  34 us
    all_to_all x1, waiting for transfers between devices, shards(): lax.all_to_all(field, 'blk', split_axis=1, concat_axis=0, tiled=True)  28.8 us
    all_to_all x1, starting transfers between devices, shards(): lax.all_to_all(field, 'blk', split_axis=1, concat_axis=0, tiled=True)  16.3 us
    cos x1, other arithmetic, filter_matrix(): table = jnp.cos(2.0 * jnp.pi * phase.astype(jnp.float32) / months)  15.4 us
  transfers between devices with their start and end apart: 3, of which 3 were waited for; matrix products, arithmetic and copies ran while one was open for 3% of the time, Pallas kernels for 0%

commit v1 on v0

v1 whole, which is shorter than its diff:
```python
import functools

import jax
import jax.numpy as jnp
import numpy as np
from jax import lax
from jax.experimental import pallas as pl
from jax.experimental.pallas import tpu as pltpu
from jax.sharding import PartitionSpec as P

MONTHS = 128
COLS = 256
ROWS = 4096
TOP = lax.Precision.HIGHEST
NY, NZ, NX = 4, 8, 4
NB = NY * NZ * NX
CHUNK = 512


def solve_lower(matrix, rhs):
    return lax.linalg.triangular_solve(matrix, rhs, left_side=True, lower=True)


def filter_matrix(response):
    months = MONTHS
    bins = response.shape[0]
    freq = np.arange(bins)
    edge = (freq == 0) | (freq == months // 2)
    coef = np.where(edge, 1.0, 2.0) / months
    angle = 2.0 * np.pi * ((np.arange(months)[:, None] * freq[None, :]) % months) / months
    cos = np.cos(angle).astype(np.float32)
    sin = np.sin(angle).astype(np.float32)
    basis = jnp.asarray(np.concatenate([cos, sin], axis=1))
    gain = jnp.asarray(coef.astype(np.float32)) * response
    return jnp.dot(basis * jnp.concatenate([gain, gain])[None, :], basis.T, precision=TOP)


def split3(value):
    high = value.astype(jnp.bfloat16)
    rest = value - high.astype(jnp.float32)
    middle = rest.astype(jnp.bfloat16)
    low = (rest - middle.astype(jnp.float32)).astype(jnp.bfloat16)
    return high, middle, low


def dot_t(a, b):
    return lax.dot_general(a, b, (((1,), (1,)), ((), ())), preferred_element_type=jnp.float32)


def gather_kernel(
    field_ref, weight_ref, f_ref, g_ref,
    fbuf, gacc, pbuf, hbuf, s1buf, s2buf, tbuf,
    own_sem, a_send, a_recv, p_send, p_recv, s1_send, s1_recv, s2_send, s2_recv, s3_send, s3_recv,
):
    core = lax.axis_index("grp")
    me = lax.axis_index("blk")
    my = me // (NZ * NX)
    mz = (me // NX) % NZ
    mx = me % NX
    mxy = my * NX + mx
    other = 1 - core

    def xy_peer(p):
        return (p // NX) * (NZ * NX) + mz * NX + p % NX

    def z_peer(p):
        return my * (NZ * NX) + p * NX + mx

    barrier = pltpu.get_barrier_semaphore()

    def greet(k, _):
        pl.semaphore_signal(barrier, inc=1, device_id={"blk": (me + k) % NB})
        return 0

    lax.fori_loop(1, NB, greet, 0)
    pl.semaphore_signal(barrier, inc=1, device_id={"grp": other})
    pl.semaphore_wait(barrier, NB)

    def cut(p):
        return field_ref.at[:, pl.ds(pl.multiple_of(p * ROWS, ROWS), ROWS)]

    def send_copy(p):
        return pltpu.make_async_remote_copy(
            src_ref=cut(p), dst_ref=fbuf.at[me], send_sem=a_send.at[p], recv_sem=a_recv.at[me],
            device_id={"blk": p})

    def recv_copy(p):
        return pltpu.make_async_remote_copy(
            src_ref=cut(p), dst_ref=fbuf.at[p], send_sem=a_send.at[p], recv_sem=a_recv.at[p],
            device_id={"blk": p})

    def send(k, _):
        send_copy((me + k) % NB).start()
        return 0

    lax.fori_loop(1, NB, send, 0)
    own = pltpu.make_async_copy(cut(me), fbuf.at[me], own_sem)
    own.start()
    gacc[...] = jnp.zeros_like(gacc)
    own.wait()

    def arrive(k, _):
        recv_copy((me + k) % NB).wait_recv()
        return 0

    lax.fori_loop(1, NB, arrive, 0)

    def gram(c, _):
        lanes = pl.ds(pl.multiple_of(c * CHUNK, CHUNK), CHUNK)
        block = fbuf[:, :, lanes].reshape(COLS, CHUNK)
        f_ref[:, lanes] = block
        w = weight_ref[:, lanes]
        weighted = block.astype(jnp.float32) * (w * w)
        high, middle, low = split3(weighted)
        gacc[...] += dot_t(block, low) + dot_t(block, middle) + dot_t(block, high)
        return 0

    lax.fori_loop(0, ROWS // CHUNK, gram, 0)

    half = COLS // 2

    def rows(start, n):
        return pl.ds(pl.multiple_of(start, n), n)

    pair = pltpu.make_async_remote_copy(
        src_ref=gacc.at[rows(other * half, half)], dst_ref=pbuf, send_sem=p_send.at[0], recv_sem=p_recv.at[0],
        device_id={"grp": other})
    pair.start()
    pair.wait()
    hbuf[...] = gacc[rows(core * half, half), :] + pbuf[...]

    def s1(p, slot):
        return pltpu.make_async_remote_copy(
            src_ref=hbuf.at[rows(p * 8, 8)], dst_ref=s1buf.at[slot], send_sem=s1_send.at[p], recv_sem=s1_recv.at[slot],
            device_id={"blk": xy_peer(p)})

    def s2(p, slot):
        return pltpu.make_async_remote_copy(
            src_ref=tbuf.at[0], dst_ref=s2buf.at[slot], send_sem=s2_send.at[p], recv_sem=s2_recv.at[slot],
            device_id={"blk": z_peer(p)})

    def s3(p, slot):
        return pltpu.make_async_remote_copy(
            src_ref=tbuf.at[1], dst_ref=g_ref.at[rows(core * half + slot * 8, 8)],
            send_sem=s3_send.at[p], recv_sem=s3_recv.at[slot], device_id={"blk": xy_peer(p)})

    for k in range(1, 16):
        s1((mxy + k) % 16, mxy).start()
    total = hbuf[rows(mxy * 8, 8), :]
    for k in range(1, 16):
        p = (mxy + k) % 16
        s1(p, p).wait_recv()
        total = total + s1buf[p]
    tbuf[0] = total
    s2buf[mz] = total
    for k in range(1, 8):
        s2((mz + k) % 8, mz).start()
    for k in range(1, 8):
        p = (mz + k) % 8
        s2(p, p).wait_recv()
    total = s2buf[0]
    for k in range(1, 8):
        total = total + s2buf[k]
    tbuf[1] = total
    g_ref[rows(core * half + mxy * 8, 8), :] = total
    for k in range(1, 16):
        s3((mxy + k) % 16, mxy).start()
    for k in range(1, 16):
        p = (mxy + k) % 16
        s3(p, p).wait_recv()
    back = pltpu.make_async_remote_copy(
        src_ref=g_ref.at[rows(core * half, half)], dst_ref=g_ref.at[rows(core * half, half)],
        send_sem=p_send.at[1], recv_sem=p_recv.at[1], device_id={"grp": other})
    back.start()
    back.wait()
    for k in range(1, 16):
        p = (mxy + k) % 16
        s1(p, p).wait_send()
        s3(p, p).wait_send()
    for k in range(1, 8):
        p = (mz + k) % 8
        s2(p, p).wait_send()

    def sent(k, _):
        send_copy((me + k) % NB).wait_send()
        return 0

    lax.fori_loop(1, NB, sent, 0)


def gather_and_gram(field, weight):
    dma = pltpu.SemaphoreType.DMA
    vmem = pl.BlockSpec(memory_space=pltpu.VMEM)
    return pl.pallas_call(
        gather_kernel,
        out_shape=(
            jax.ShapeDtypeStruct((COLS, ROWS), jnp.bfloat16),
            jax.ShapeDtypeStruct((COLS, COLS), jnp.float32),
        ),
        in_specs=[pl.BlockSpec(memory_space=pl.ANY), vmem],
        out_specs=(vmem, vmem),
        scratch_shapes=[
            pltpu.VMEM((NB, 2, ROWS), jnp.bfloat16),
            pltpu.VMEM((COLS, COLS), jnp.float32),
            pltpu.VMEM((COLS // 2, COLS), jnp.float32),
            pltpu.VMEM((COLS // 2, COLS), jnp.float32),
            pltpu.VMEM((16, 8, COLS), jnp.float32),
            pltpu.VMEM((8, 8, COLS), jnp.float32),
            pltpu.VMEM((2, 8, COLS), jnp.float32),
            dma, dma((NB,)), dma((NB,)), dma((2,)), dma((2,)),
            dma((16,)), dma((16,)), dma((8,)), dma((8,)), dma((16,)), dma((16,)),
        ],
        compiler_params=pltpu.CompilerParams(
            collective_id=0, has_side_effects=True, vmem_limit_bytes=40 * 1024 * 1024),
        name="gather_gram",
    )(field, weight)


def shards(field, response, area_weight):
    weight = area_weight.reshape(1, ROWS)
    gathered, raw = gather_and_gram(field, weight)
    total = jnp.float32(ROWS * lax.axis_size("grp") * lax.axis_size("blk"))
    mixing = filter_matrix(response)
    zero = jnp.zeros_like(mixing)
    both = jnp.concatenate(
        [jnp.concatenate([mixing, zero], axis=1), jnp.concatenate([zero, mixing], axis=1)], axis=0)
    gram = jnp.dot(jnp.dot(both, raw / total, precision=TOP), both.T, precision=TOP)
    lower = jnp.linalg.cholesky(gram)
    solver = solve_lower(lower, both)
    patterns = jnp.dot(solver, gathered.astype(jnp.float32), precision=TOP) * weight
    return patterns, lower.T


def solution(mesh):
    in_specs = (P("blk", "grp"), P(), P(("grp", "blk")))
    out_specs = (P(None, ("grp", "blk")), P())
    return jax.shard_map(shards, mesh=mesh, in_specs=in_specs, out_specs=out_specs, check_vma=False)
```

time: 755 us -> 163 us (0.22); the launches traced: 744 us -> 163 us
  waiting for transfers between devices: 528 us -> 0 us
  Pallas kernels: 0 us -> 92.1 us
  other arithmetic: 133 us -> 54.6 us
  matrix products: 33.7 us -> 7.21 us
  starting transfers between devices: 16.6 us -> 0 us
  between operations: 17.1 us -> 2.01 us
  local copies, waits for them, and re-layouts: 15.1 us -> 7.13 us
    psum x2 -> x0, waiting for transfers between devices: 499 us -> none  [global_gram(): return lax.psum(matrix, ('grp', 'blk'))]
    pallas_call x0 -> x1, Pallas kernels: none -> 92.1 us  [gather_and_gram(): pl.pallas_call(gather_kernel, out_shape=(jax.ShapeDtypeStruct((COLS, ROWS...]
    another operation x13 -> x6, other arithmetic: 68.9 us -> 33.9 us  [shards(): lower = jnp.linalg.cholesky(gram)]
    all_to_all x1 -> x0, waiting for transfers between devices: 28.8 us -> none  [shards(): lax.all_to_all(field, 'blk', split_axis=1, concat_axis=0, tiled=True)]
    another operation x4 -> x2, other arithmetic: 39.8 us -> 19.9 us  [solve_lower(): return lax.linalg.triangular_solve(matrix, rhs, left_side=True, lower=True)]
    all_to_all x1 -> x0, starting transfers between devices: 16.3 us -> none  [shards(): lax.all_to_all(field, 'blk', split_axis=1, concat_axis=0, tiled=True)]
    cos x1 -> x0, other arithmetic: 15.4 us -> none  [filter_matrix(): table = jnp.cos(2.0 * jnp.pi * phase.astype(jnp.float32) / months)]
    another operation x6 -> x3, matrix products: 15 us -> 0.86 us  [solve_lower(): return lax.linalg.triangular_solve(matrix, rhs, left_side=True, lower=True)]
  transfers between devices with their start and end apart: 3 -> 0, of which waited for: 3 -> 0; matrix products, arithmetic and copies ran while one was open for 3% -> 0% of each run, Pallas kernels for 0% -> 0%
where the time goes in v1:
time: 163 us
  Pallas kernels  92.1 us (57%)
  other arithmetic  54.6 us (33%)
  matrix products  7.21 us (4%)
  local copies, waits for them, and re-layouts  7.13 us (4%)
  between operations  2.01 us (1%)
    pallas_call x1, Pallas kernels, gather_and_gram(): pl.pallas_call(gather_kernel, out_shape=(jax.ShapeDtypeStruct((COLS, ROWS...  92.1 us
    another operation x6, other arithmetic, shards(): lower = jnp.linalg.cholesky(gram)  33.9 us
    another operation x2, other arithmetic, solve_lower(): return lax.linalg.triangular_solve(matrix, rhs, left_side=True, lower=True)  19.9 us
    dot_general x1, matrix products, shards(): jnp.dot(solver, gathered.astype(jnp.float32), precision=TOP) * weight  3.82 us
    another operation x6, local copies, waits for them, and re-layouts  3.74 us

profile of v1, /device:TPU:1, one launch (start us, length us, event | category | flops | bytes accessed | tf_op | source)
XLA Modules:
  0.0 163.2 jit_solution(12430339019786198104)
XLA Ops:
  0.6 0.7 mul.19
  1.3 0.1 pad_maximum_fusion.3
  1.4 0.1 triangular_solve.53
  1.5 1.3 fusion.10
  2.8 0.0 copy-start
  2.8 1.6 copy-done
  4.4 0.0 copy-start.1
  4.4 0.7 copy-done.1
  5.1 92.1 %gather_gram.1 = (bf16[256,4096]{1,0:T(8,128)(2,1)S(1)}, f32[256,256]{1,0:T(8,128)S(1)}) custom-call(bf16[2,524288]{1,0:T(2,128)(2,1)S(1)} %copy-done, f32[1,4096]{1,0:T(1,128)S(1)} %bitcast.37), custom_call_target="tpu_custom_call" | custom-call | tf_op jit(solution)/shard_map/gather_gram/pallas_call | solution.py:194
  97.2 0.4 fusion.4
  97.6 0.4 fusion.8
  98.0 0.1 copy.7
  98.2 11.7 %cholesky.49 = f32[128,128]{1,0:T(8,128)S(1)} custom-call(f32[128,128]{1,0:T(8,128)S(1)} %cholesky.115), custom_call_target="Cholesky" | custom-call | tf_op jit(solution)/shard_map/jit(cholesky)/cholesky | solution.py:228
  110.0 0.0 copy-start.2
  110.0 9.8 %custom-call.14 = f32[1,128,128]{1,2,0:T(8,128)S(1)} custom-call(f32[1,128,128]{2,1,0:T(8,128)S(1)} %get-tuple-element.31), custom_call_target="InvertDiagBlocksLowerTriangular" | custom-call | tf_op jit(solution)/shard_map/jit(cholesky)/cholesky | solution.py:228
  119.8 0.2 constant_dynamic-update-slice_fusion.1
  120.0 0.3 convolution_subtract_fusion.1
  120.3 11.7 %cholesky.102 = f32[128,128]{1,0:T(8,128)S(1)} custom-call(f32[128,128]{1,0:T(8,128)S(1)} %convolution_subtract_fusion.1), custom_call_target="Cholesky" | custom-call | tf_op jit(solution)/shard_map/jit(cholesky)/cholesky | solution.py:228
  132.1 0.6 compare_reduce_fusion
  134.0 0.8 copy.8
  134.8 3.8 %while.1 = (s32[]{:T(128)}, f32[256,256]{1,0:T(8,128)S(1)}, s32[2,2]{1,0:T(2,128)S(1)}, f32[2,128,128]{2,1,0:T(8,128)S(1)}, s32[]{:T(128)}) while((s32[]{:T(128)}, f32[256,256]{1,0:T(8,128)S(1)}, s32[2,2]{1,0:T(2,128)S(1)}, f32[2,128,128]{2,1,0:T(8,128)S(1)}, s32[]{:T(128)}) %tuple.30), condition=%wide.while_cond, body=%wide.while_body.sunk | while | flops 2 | bytes 131189 | solution.py:21
  134.8 0.6 fusion.35
  135.4 1.3 bitcast_dynamic-update-slice_fusion.2
  136.7 0.6 fusion.35
  137.3 1.3 bitcast_dynamic-update-slice_fusion.2
  138.6 19.9 %custom-call.15 = f32[2,128,128]{1,2,0:T(8,128)S(1)} custom-call(f32[2,128,128]{2,1,0:T(8,128)S(1)} %get-tuple-element.13), custom_call_target="InvertDiagBlocksLowerTriangular" | custom-call | tf_op jit(solution)/shard_map/triangular_solve | solution.py:21
  158.4 0.3 fusion.14
  158.7 0.3 convolution_subtract_fusion
  159.0 0.3 fusion.13
  159.3 0.0 copy-done.2
  159.3 3.8 %convolution_multiply_fusion = f32[256,4096]{1,0:T(8,128)} fusion(bf16[256,4096]{1,0:T(8,128)(2,1)S(1)} %get-tuple-element.5, f32[4096]{0:T(1024)S(1)} %copy-done.2, f32[128,256]{1,0:T(8,128)S(1)} %fusion.13, f32[128,256]{1,0:T(8,128)S(1)} %fusion.14), kind=kOutput, calls=%fused_computation.2 | convolution fusion | flops 3222339584 | bytes 6569984 | tf_op jit(solution)/shard_map/dot_general | solution.py:230
  (11 shorter events, 0.2 us)
Async XLA Ops:
  2.8 1.6 copy-start
  4.4 0.7 copy-start.1
  110.0 49.3 %copy-start.2 = (f32[4096]{0:T(1024)S(1)}, f32[4096]{0:T(1024)}, u32[]{:S(2)}) copy-start(f32[4096]{0:T(1024)} %param.7) | copy-start | bytes 49156

commit v2 on v1

--- a/solution.py
+++ b/solution.py
@@ -1,5 +1,3 @@
-import functools
-
 import jax
 import jax.numpy as jnp
 import numpy as np
@@ -10,29 +8,25 @@
 
 MONTHS = 128
 COLS = 256
+BINS = MONTHS // 2 + 1
 ROWS = 4096
+POINTS = 1048576
 TOP = lax.Precision.HIGHEST
 NY, NZ, NX = 4, 8, 4
 NB = NY * NZ * NX
 CHUNK = 512
-
-
-def solve_lower(matrix, rhs):
-    return lax.linalg.triangular_solve(matrix, rhs, left_side=True, lower=True)
-
-
-def filter_matrix(response):
-    months = MONTHS
-    bins = response.shape[0]
-    freq = np.arange(bins)
-    edge = (freq == 0) | (freq == months // 2)
-    coef = np.where(edge, 1.0, 2.0) / months
-    angle = 2.0 * np.pi * ((np.arange(months)[:, None] * freq[None, :]) % months) / months
-    cos = np.cos(angle).astype(np.float32)
-    sin = np.sin(angle).astype(np.float32)
-    basis = jnp.asarray(np.concatenate([cos, sin], axis=1))
-    gain = jnp.asarray(coef.astype(np.float32)) * response
-    return jnp.dot(basis * jnp.concatenate([gain, gain])[None, :], basis.T, precision=TOP)
+BLOCK = 16
+WIDE = 384
+OUT_CHUNK = 512
+
+
+def filter_tables():
+    freq = np.arange(BINS)
+    edge = (freq == 0) | (freq == MONTHS // 2)
+    coef = np.where(edge, 1.0, 2.0) / MONTHS
+    angle = 2.0 * np.pi * ((np.arange(MONTHS)[:, None] * freq[None, :]) % MONTHS) / MONTHS
+    cos, sin = np.cos(angle), np.sin(angle)
+    return np.stack([cos, sin, cos * coef, sin * coef]).astype(np.float32)
 
 
 def split3(value):
@@ -43,12 +37,135 @@
     return high, middle, low
 
 
-def dot_t(a, b):
-    return lax.dot_general(a, b, (((1,), (1,)), ((), ())), preferred_element_type=jnp.float32)
+def dot_t(a, b, precision=None):
+    return lax.dot_general(a, b, (((1,), (1,)), ((), ())), precision=precision, preferred_element_type=jnp.float32)
+
+
+def row_of(tile, s):
+    return jnp.broadcast_to(tile[s:s + 1, :], (8, 128))
+
+
+def eliminate(work):
+    sub = lax.broadcasted_iota(jnp.int32, (8, 128), 0)
+    for b in range(COLS // BLOCK):
+        r0 = b * BLOCK
+        base = 0 if r0 < MONTHS else MONTHS
+        lane = r0 - base
+        top = [work[r0:r0 + 8, base + 128 * t:base + 128 * t + 128] for t in range(3)]
+        bot = [work[r0 + 8:r0 + 16, base + 128 * t:base + 128 * t + 128] for t in range(3)]
+        ct = [jnp.broadcast_to(top[0][:, lane + j:lane + j + 1], (8, 128)) for j in range(8)]
+        cb = [jnp.broadcast_to(bot[0][:, lane + j:lane + j + 1], (8, 128)) for j in range(16)]
+        for j in range(BLOCK):
+            if j < 8:
+                d = lax.rsqrt(row_of(ct[j], j))
+                lt = jnp.where(sub > j, ct[j] * d, 0.0)
+                lb = cb[j] * d
+                for k in range(j + 1, 8):
+                    f = row_of(lt, k)
+                    ct[k] = ct[k] - lt * f
+                    cb[k] = cb[k] - lb * f
+                for k in range(8, 16):
+                    cb[k] = cb[k] - lb * row_of(lb, k - 8)
+                for t in range(3):
+                    u = row_of(top[t], j) * d
+                    bot[t] = bot[t] - lb * u
+                    top[t] = jnp.where(sub == j, u, top[t] - lt * u)
+            else:
+                i = j - 8
+                d = lax.rsqrt(row_of(cb[j], i))
+                lb = jnp.where(sub > i, cb[j] * d, 0.0)
+                for k in range(j + 1, 16):
+                    cb[k] = cb[k] - lb * row_of(lb, k - 8)
+                for t in range(3):
+                    u = row_of(bot[t], i) * d
+                    bot[t] = jnp.where(sub == i, u, bot[t] - lb * u)
+        for t in range(3):
+            work[r0:r0 + 8, base + 128 * t:base + 128 * t + 128] = top[t]
+            work[r0 + 8:r0 + 16, base + 128 * t:base + 128 * t + 128] = bot[t]
+        nxt = r0 + BLOCK
+        if nxt < COLS:
+            panel = jnp.concatenate([jnp.concatenate(top, axis=1), jnp.concatenate(bot, axis=1)], axis=0)
+            h, m, l = split3(panel)
+            first = nxt // 128 * 128
+            left = first - base
+            width = COLS - first
+            cut = lambda x: x[:, left:left + width]
+            a = jnp.concatenate([cut(h), cut(h), cut(m), cut(h), cut(l), cut(m)], axis=0)
+            c = jnp.concatenate([h, m, h, l, h, m], axis=0)
+            prod = lax.dot_general(a, c, (((0,), (0,)), ((), ())), preferred_element_type=jnp.float32)
+            work[nxt:COLS, base:base + WIDE] = work[nxt:COLS, base:base + WIDE] - prod[nxt - first:, :]
+
+
+def solve_kernel(raw_ref, filt_ref, weight_ref, f_ref, out_ref, r_ref, work, fbuf, obuf, fsem, osem):
+    load = pltpu.make_async_copy(f_ref, fbuf, fsem)
+    load.start()
+    mix = filt_ref[...]
+    half = MONTHS
+    scaled = raw_ref[...] * (1.0 / POINTS)
+
+    def side(block):
+        return jnp.dot(mix, dot_t(block, mix, TOP), precision=TOP, preferred_element_type=jnp.float32)
+
+    zero = jnp.zeros((half, half), jnp.float32)
+    work[:half, :half] = side(scaled[:half, :half])
+    work[:half, half:2 * half] = side(scaled[:half, half:])
+    work[half:, half:2 * half] = side(scaled[half:, half:])
+    work[half:, :half] = zero
+    work[:half, 2 * half:3 * half] = mix
+    work[:half, 3 * half:] = zero
+    work[half:, 2 * half:3 * half] = zero
+    work[half:, 3 * half:] = mix
+    eliminate(work)
+    r = lax.broadcasted_iota(jnp.int32, (COLS, COLS), 0)
+    c = lax.broadcasted_iota(jnp.int32, (COLS, COLS), 1)
+    r_ref[...] = jnp.where(r <= c, work[:, :COLS], 0.0)
+    th, tm, tl = split3(work[:, COLS:])
+    load.wait()
+    n = ROWS // OUT_CHUNK
+
+    def put(i):
+        return pltpu.make_async_copy(
+            obuf.at[i], out_ref.at[:, pl.ds(pl.multiple_of(i * OUT_CHUNK, OUT_CHUNK), OUT_CHUNK)], osem.at[i])
+
+    def chunk(i, _):
+        lanes = pl.ds(pl.multiple_of(i * OUT_CHUNK, OUT_CHUNK), OUT_CHUNK)
+        f = fbuf[:, lanes]
+        dot = lambda t: jnp.dot(t, f, preferred_element_type=jnp.float32)
+        obuf[i] = (dot(tl) + dot(tm) + dot(th)) * weight_ref[:, lanes]
+        put(i).start()
+        return 0
+
+    lax.fori_loop(0, n, chunk, 0)
+
+    def done(i, _):
+        put(i).wait()
+        return 0
+
+    lax.fori_loop(0, n, done, 0)
+
+
+def solve(raw, filt, weight, gathered):
+    vmem = pl.BlockSpec(memory_space=pltpu.VMEM)
+    hbm = pl.BlockSpec(memory_space=pl.ANY)
+    n = ROWS // OUT_CHUNK
+    return pl.pallas_call(
+        solve_kernel,
+        out_shape=(jax.ShapeDtypeStruct((COLS, ROWS), jnp.float32), jax.ShapeDtypeStruct((COLS, COLS), jnp.float32)),
+        in_specs=[vmem, vmem, vmem, hbm],
+        out_specs=(hbm, vmem),
+        scratch_shapes=[
+            pltpu.VMEM((COLS, 4 * MONTHS), jnp.float32),
+            pltpu.VMEM((COLS, ROWS), jnp.bfloat16),
+            pltpu.VMEM((n, COLS, OUT_CHUNK), jnp.float32),
+            pltpu.SemaphoreType.DMA, pltpu.SemaphoreType.DMA((n,)),
+        ],
+        compiler_params=pltpu.CompilerParams(vmem_limit_bytes=60 * 1024 * 1024),
+        name="solve",
+    )(raw, filt, weight, gathered)
 
 
 def gather_kernel(
-    field_ref, weight_ref, f_ref, g_ref,
+    field_ref, weight_ref, response_ref, table_ref, f_ref, g_ref, filt_ref,
     fbuf, gacc, pbuf, hbuf, s1buf, s2buf, tbuf,
     own_sem, a_send, a_recv, p_send, p_recv, s1_send, s1_recv, s2_send, s2_recv, s3_send, s3_recv,
 ):
@@ -97,6 +214,9 @@
     own = pltpu.make_async_copy(cut(me), fbuf.at[me], own_sem)
     own.start()
     gacc[...] = jnp.zeros_like(gacc)
+    gain = response_ref[...]
+    filt_ref[...] = (
+        dot_t(table_ref[2] * gain, table_ref[0], TOP) + dot_t(table_ref[3] * gain, table_ref[1], TOP))
     own.wait()
 
     def arrive(k, _):
@@ -188,7 +308,7 @@
     lax.fori_loop(1, NB, sent, 0)
 
 
-def gather_and_gram(field, weight):
+def gather_and_gram(field, weight, response, table):
     dma = pltpu.SemaphoreType.DMA
     vmem = pl.BlockSpec(memory_space=pltpu.VMEM)
     return pl.pallas_call(
@@ -196,9 +316,10 @@
         out_shape=(
             jax.ShapeDtypeStruct((COLS, ROWS), jnp.bfloat16),
             jax.ShapeDtypeStruct((COLS, COLS), jnp.float32),
+            jax.ShapeDtypeStruct((MONTHS, MONTHS), jnp.float32),
         ),
-        in_specs=[pl.BlockSpec(memory_space=pl.ANY), vmem],
-        out_specs=(vmem, vmem),
+        in_specs=[pl.BlockSpec(memory_space=pl.ANY), vmem, vmem, vmem],
+        out_specs=(vmem, vmem, vmem),
         scratch_shapes=[
             pltpu.VMEM((NB, 2, ROWS), jnp.bfloat16),
             pltpu.VMEM((COLS, COLS), jnp.float32),
@@ -211,24 +332,15 @@
             dma((16,)), dma((16,)), dma((8,)), dma((8,)), dma((16,)), dma((16,)),
         ],
         compiler_params=pltpu.CompilerParams(
-            collective_id=0, has_side_effects=True, vmem_limit_bytes=40 * 1024 * 1024),
+            collective_id=0, has_side_effects=True, vmem_limit_bytes=60 * 1024 * 1024),
         name="gather_gram",
-    )(field, weight)
+    )(field, weight, response, table)
 
 
 def shards(field, response, area_weight):
     weight = area_weight.reshape(1, ROWS)
-    gathered, raw = gather_and_gram(field, weight)
-    total = jnp.float32(ROWS * lax.axis_size("grp") * lax.axis_size("blk"))
-    mixing = filter_matrix(response)
-    zero = jnp.zeros_like(mixing)
-    both = jnp.concatenate(
-        [jnp.concatenate([mixing, zero], axis=1), jnp.concatenate([zero, mixing], axis=1)], axis=0)
-    gram = jnp.dot(jnp.dot(both, raw / total, precision=TOP), both.T, precision=TOP)
-    lower = jnp.linalg.cholesky(gram)
-    solver = solve_lower(lower, both)
-    patterns = jnp.dot(solver, gathered.astype(jnp.float32), precision=TOP) * weight
-    return patterns, lower.T
+    gathered, raw, filt = gather_and_gram(field, weight, response.reshape(1, BINS), jnp.asarray(filter_tables()))
+    return solve(raw, filt, weight, gathered)
 
 
 def solution(mesh):

time: 163 us -> 110 us (0.67)
  other arithmetic: 54.6 us -> 0 us
  Pallas kernels: 92.1 us -> 109 us
  matrix products: 7.21 us -> 0 us
  local copies, waits for them, and re-layouts: 7.13 us -> 0 us
    another operation x8 -> x0, other arithmetic: 53.8 us -> none  [the longest x6 33.9 us: shards(): lower = jnp.linalg.cholesky(gram)]
    pallas_call x0 -> x1, Pallas kernels: none -> 14 us  [solve(): pl.pallas_call(solve_kernel, out_shape=(jax.ShapeDtypeStruct((COLS, ROWS)...]
    dot_general x4 -> x0, matrix products: 5.88 us -> none  [the longest x1 3.82 us: shards(): jnp.dot(solver, gathered.astype(jnp.float32), precision=TOP) * weight]
    another operation x9 -> x0, local copies, waits for them, and re-layouts: 3.83 us -> none
    unnamed x7 -> x0, local copies, waits for them, and re-layouts: 3.14 us -> none
    pallas_call x1, Pallas kernels: 92.1 us -> 94.9 us  [gather_and_gram(): pl.pallas_call(gather_kernel, out_shape=(jax.ShapeDtypeStruct((COLS, ROWS...]
where the time goes in v2:
time: 110 us
  Pallas kernels  109 us (99%)
    pallas_call x1, Pallas kernels, gather_and_gram(): pl.pallas_call(gather_kernel, out_shape=(jax.ShapeDtypeStruct((COLS, ROWS...  94.9 us
    pallas_call x1, Pallas kernels, solve(): pl.pallas_call(solve_kernel, out_shape=(jax.ShapeDtypeStruct((COLS, ROWS)...  14 us

profile of v2, /device:TPU:1, one launch (start us, length us, event | category | flops | bytes accessed | tf_op | source)
XLA Modules:
  0.0 109.6 jit_solution(17974299141438313949)
XLA Ops:
  0.6 94.9 %gather_gram.1 = (bf16[256,4096]{1,0:T(8,128)(2,1)}, f32[256,256]{1,0:T(8,128)}, f32[128,128]{1,0:T(8,128)}) custom-call(bf16[2,524288]{1,0:T(2,128)(2,1)} %field_ref.1, f32[1,4096]{1,0:T(1,128)} %bitcast.2, f32[1,65]{1,0:T(1,128)} %bitcast.4, f32[4,128,65]{2,1,0:T(8,128)} %constant.2.clone.table_ref), custom_call_target="tpu_custom_call" | custom-call | tf_op jit(solution)/shard_map/gather_gram/pallas_call | solution.py:314
  95.5 14.0 %solve.1 = (f32[256,4096]{1,0:T(8,128)}, f32[256,256]{1,0:T(8,128)}) custom-call(f32[256,256]{1,0:T(8,128)} %get-tuple-element.5.raw_ref, f32[128,128]{1,0:T(8,128)} %get-tuple-element.6.filt_ref, f32[1,4096]{1,0:T(1,128)} %bitcast.3, bf16[256,4096]{1,0:T(8,128)(2,1)} %get-tuple-element.7.f_ref), custom_call_target="tpu_custom_call" | custom-call | tf_op jit(solution)/shard_map/solve/pallas_call | solution.py:151

commit v3 on v0

v3 whole, which is shorter than its diff:
```python
import jax
import jax.numpy as jnp
import numpy as np
from jax import lax
from jax.experimental import pallas as pl
from jax.experimental.pallas import tpu as pltpu
from jax.sharding import PartitionSpec as P

MONTHS = 128
COLS = 256
BINS = MONTHS // 2 + 1
ROWS = 4096
POINTS = 1048576
TOP = lax.Precision.HIGHEST
NY, NZ, NX = 4, 8, 4
NB = NY * NZ * NX
PLANE = NZ * NX
GROUP = 2 * PLANE
CHUNK = 1024
BLOCK = 16
WIDE = 384
OUT_CHUNK = 512
OUT_STEPS = ROWS // OUT_CHUNK


def filter_tables():
    freq = np.arange(BINS)
    edge = (freq == 0) | (freq == MONTHS // 2)
    coef = np.where(edge, 1.0, 2.0) / MONTHS
    angle = 2.0 * np.pi * ((np.arange(MONTHS)[:, None] * freq[None, :]) % MONTHS) / MONTHS
    cos, sin = np.cos(angle), np.sin(angle)
    return np.stack([cos, sin, cos * coef, sin * coef]).astype(np.float32)


def split3(value):
    high = value.astype(jnp.bfloat16)
    rest = value - high.astype(jnp.float32)
    middle = rest.astype(jnp.bfloat16)
    low = (rest - middle.astype(jnp.float32)).astype(jnp.bfloat16)
    return high, middle, low


def dot_t(a, b, precision=None):
    return lax.dot_general(a, b, (((1,), (1,)), ((), ())), precision=precision, preferred_element_type=jnp.float32)


def aligned(start, n):
    return pl.ds(pl.multiple_of(start, n), n)


def row_of(tile, s):
    return jnp.broadcast_to(tile[s:s + 1, :], (8, 128))


def eliminate(work, b):
    sub = lax.broadcasted_iota(jnp.int32, (8, 128), 0)
    r0 = b * BLOCK
    base = 0 if r0 < MONTHS else MONTHS
    lane = r0 - base
    top = [work[r0:r0 + 8, base + 128 * t:base + 128 * t + 128] for t in range(3)]
    bot = [work[r0 + 8:r0 + 16, base + 128 * t:base + 128 * t + 128] for t in range(3)]
    ct = [jnp.broadcast_to(top[0][:, lane + j:lane + j + 1], (8, 128)) for j in range(8)]
    cb = [jnp.broadcast_to(bot[0][:, lane + j:lane + j + 1], (8, 128)) for j in range(16)]
    for j in range(BLOCK):
        if j < 8:
            d = lax.rsqrt(row_of(ct[j], j))
            lt = jnp.where(sub > j, ct[j] * d, 0.0)
            lb = cb[j] * d
            for k in range(j + 1, 8):
                f = row_of(lt, k)
                ct[k] = ct[k] - lt * f
                cb[k] = cb[k] - lb * f
            for k in range(8, 16):
                cb[k] = cb[k] - lb * row_of(lb, k - 8)
            for t in range(3):
                u = row_of(top[t], j) * d
                bot[t] = bot[t] - lb * u
                top[t] = jnp.where(sub == j, u, top[t] - lt * u)
        else:
            i = j - 8
            d = lax.rsqrt(row_of(cb[j], i))
            lb = jnp.where(sub > i, cb[j] * d, 0.0)
            for k in range(j + 1, 16):
                cb[k] = cb[k] - lb * row_of(lb, k - 8)
            for t in range(3):
                u = row_of(bot[t], i) * d
                bot[t] = jnp.where(sub == i, u, bot[t] - lb * u)
    for t in range(3):
        work[r0:r0 + 8, base + 128 * t:base + 128 * t + 128] = top[t]
        work[r0 + 8:r0 + 16, base + 128 * t:base + 128 * t + 128] = bot[t]
    nxt = r0 + BLOCK
    if nxt == COLS:
        return
    panel = jnp.concatenate([jnp.concatenate(top, axis=1), jnp.concatenate(bot, axis=1)], axis=0)
    h, m, l = split3(panel)
    first = nxt // 128 * 128
    left = first - base
    width = COLS - first
    cut = lambda x: x[:, left:left + width]
    a = jnp.concatenate([cut(h), cut(h), cut(m), cut(h), cut(l), cut(m)], axis=0)
    c = jnp.concatenate([h, m, h, l, h, m], axis=0)
    prod = lax.dot_general(a, c, (((0,), (0,)), ((), ())), preferred_element_type=jnp.float32)
    work[nxt:COLS, base:base + WIDE] = work[nxt:COLS, base:base + WIDE] - prod[nxt - first:, :]


def solve_kernel(raw_ref, filt_ref, weight_ref, f_ref, out_ref, r_ref, work, obuf, osem):
    mix = filt_ref[...]
    half = MONTHS

    def side(block):
        return jnp.dot(mix, dot_t(block, mix, TOP), precision=TOP, preferred_element_type=jnp.float32)

    def fold(i, j):
        first = raw_ref[i * half:(i + 1) * half, j * half:(j + 1) * half]
        second = raw_ref[j * half:(j + 1) * half, i * half:(i + 1) * half]
        return (first + second.T) * (1.0 / POINTS)

    zero = jnp.zeros((half, half), jnp.float32)
    work[:half, :half] = side(fold(0, 0))
    work[:half, half:2 * half] = side(fold(0, 1))
    work[half:, half:2 * half] = side(fold(1, 1))
    work[half:, :half] = zero
    work[:half, 2 * half:3 * half] = mix
    work[:half, 3 * half:] = zero
    work[half:, 2 * half:3 * half] = zero
    work[half:, 3 * half:] = mix

    def put(i, k):
        return pltpu.make_async_copy(
            obuf.at[i, aligned(k * half, half)],
            out_ref.at[aligned(k * half, half), aligned(i * OUT_CHUNK, OUT_CHUNK)], osem.at[k, i])

    def project(i, k, terms, depth):
        lanes = aligned(i * OUT_CHUNK, OUT_CHUNK)
        f = f_ref[:depth, lanes]
        dot = lambda t: jnp.dot(t, f, preferred_element_type=jnp.float32)
        high, middle, low = terms
        obuf[i, k * half:(k + 1) * half, :] = (dot(low) + dot(middle) + dot(high)) * weight_ref[:, lanes]
        put(i, k).start()

    for b in range(8):
        eliminate(work, b)
    upper = split3(work[:half, 2 * half:3 * half])
    for b in range(8, 16):
        eliminate(work, b)
        project(b - 8, 0, upper, half)
    lower = split3(work[half:, 2 * half:])

    def step(i, _):
        project(i, 1, lower, COLS)
        return 0

    lax.fori_loop(0, OUT_STEPS, step, 0)
    r = lax.broadcasted_iota(jnp.int32, (COLS, COLS), 0)
    c = lax.broadcasted_iota(jnp.int32, (COLS, COLS), 1)
    r_ref[...] = jnp.where(r <= c, work[:, :COLS], 0.0)

    def done(i, _):
        put(i, 0).wait()
        put(i, 1).wait()
        return 0

    lax.fori_loop(0, OUT_STEPS, done, 0)


def solve(raw, filt, weight, gathered):
    vmem = pl.BlockSpec(memory_space=pltpu.VMEM)
    hbm = pl.BlockSpec(memory_space=pltpu.HBM)
    return pl.pallas_call(
        solve_kernel,
        out_shape=(jax.ShapeDtypeStruct((COLS, ROWS), jnp.float32), jax.ShapeDtypeStruct((COLS, COLS), jnp.float32)),
        in_specs=[vmem, vmem, vmem, vmem],
        out_specs=(hbm, vmem),
        scratch_shapes=[
            pltpu.VMEM((COLS, 4 * MONTHS), jnp.float32),
            pltpu.VMEM((OUT_STEPS, COLS, OUT_CHUNK), jnp.float32),
            pltpu.SemaphoreType.DMA((2, OUT_STEPS)),
        ],
        compiler_params=pltpu.CompilerParams(vmem_limit_bytes=16 * 1024 * 1024),
        name="solve",
    )(raw, filt, weight, gathered)


def gather_kernel(
    field_ref, weight_in, response_in, table_in, f_ref, g_ref, filt_ref, weight_ref,
    response_ref, table_ref, fbuf, gacc, terms, pbuf, hbuf, s1buf, s2buf, tbuf,
    phase, own_sem, a_send, a_recv, p_send, p_recv, s1_send, s1_recv, s2_send, s2_recv, s3_send, s3_recv,
):
    core = lax.axis_index("grp")
    me = lax.axis_index("blk")
    my = me // PLANE
    mz = (me // NX) % NZ
    mx = me % NX
    mxy = my * NX + mx
    other = 1 - core

    def at(y, z, x):
        return (y % NY) * PLANE + (z % NZ) * NX + x % NX

    def xy_peer(p):
        return at(p // NX, mz, p % NX)

    def signal(sem, **where):
        pl.semaphore_signal(sem, inc=1, device_id=where)

    def cut(p):
        return field_ref.at[:, aligned(p * ROWS, ROWS)]

    def copy(p, slot):
        return pltpu.make_async_remote_copy(
            src_ref=cut(p), dst_ref=fbuf.at[slot], send_sem=a_send.at[p], recv_sem=a_recv.at[slot],
            device_id={"blk": p})

    barrier = pltpu.get_barrier_semaphore()
    for k in range(1, NZ):
        signal(barrier, blk=at(my, mz + k, mx))
    for k in range(1, NX):
        signal(barrier, blk=at(my, mz, mx + k))
    for k in range(1, NY):
        signal(barrier, blk=at(my + k, mz, mx))
    signal(barrier, grp=other)
    pl.semaphore_wait(barrier, NZ + NX + NY - 2)
    for k in range(1, NX):
        signal(phase.at[0], blk=at(my, mz, mx + k))

    def send_line(i, _):
        copy(at(my, mz + i, mx), me).start()
        return 0

    lax.fori_loop(1, NZ, send_line, 0)
    local = [
        pltpu.make_async_copy(cut(me), fbuf.at[me], own_sem.at[0]),
        pltpu.make_async_copy(weight_in, weight_ref, own_sem.at[1]),
        pltpu.make_async_copy(response_in, response_ref, own_sem.at[2]),
        pltpu.make_async_copy(table_in, table_ref, own_sem.at[3]),
    ]
    for each in local:
        each.start()
    pl.semaphore_wait(phase.at[0], NX - 1)
    for k in range(1, NY):
        signal(phase.at[1], blk=at(my + k, mz, mx))

    def send_plane(i, _):
        copy(at(my, mz + i % NZ, mx + 1 + i // NZ), me).start()
        return 0

    lax.fori_loop(0, PLANE - NZ, send_plane, 0)
    pl.semaphore_wait(phase.at[1], NY - 1)

    def send_rest(i, _):
        copy(at(my + 1 + i // PLANE, mz + i % NZ, mx + (i // NZ) % NX), me).start()
        return 0

    lax.fori_loop(0, NB - PLANE, send_rest, 0)

    f_ref[...] = jnp.zeros_like(f_ref)
    for each in local:
        each.wait()
    gain = response_ref[...]
    filt_ref[...] = (
        dot_t(table_ref[2] * gain, table_ref[0], TOP) + dot_t(table_ref[3] * gain, table_ref[1], TOP))

    def window(t, _):
        group = (my + NY - t) % NY

        def arrive(i, _):
            p = group * PLANE + (mz * NX + mx + i) % PLANE
            copy(p, p).wait_recv()
            return 0

        lax.fori_loop(jnp.where(t == 0, 1, 0), PLANE, arrive, 0)
        rows = aligned(group * GROUP, GROUP)
        terms[...] = jnp.zeros_like(terms)

        def gram(c, _):
            lanes = aligned(c * CHUNK, CHUNK)
            block = fbuf[aligned(group * PLANE, PLANE), :, lanes].reshape(GROUP, CHUNK)
            f_ref[rows, lanes] = block
            w = weight_ref[:, lanes]
            pieces = jnp.concatenate(split3(block.astype(jnp.float32) * (w * w)), axis=0)
            terms[...] += dot_t(pieces, f_ref[:, lanes])
            return 0

        lax.fori_loop(0, ROWS // CHUNK, gram, 0)
        total = terms[2 * GROUP:, :] + terms[GROUP:2 * GROUP, :] + terms[:GROUP, :]
        column = lax.broadcasted_iota(jnp.int32, (GROUP, COLS), 1)
        gacc[rows, :] = jnp.where(column // GROUP == group, 0.5 * total, total)
        return 0

    lax.fori_loop(0, NY, window, 0)

    half = COLS // 2
    pair = pltpu.make_async_remote_copy(
        src_ref=gacc.at[aligned(other * half, half)], dst_ref=pbuf, send_sem=p_send, recv_sem=p_recv,
        device_id={"grp": other})
    pair.start()
    pair.wait()
    hbuf[...] = gacc[aligned(core * half, half), :] + pbuf[...]

    def s1(p, slot):
        return pltpu.make_async_remote_copy(
            src_ref=hbuf.at[aligned(p * 8, 8)], dst_ref=s1buf.at[slot], send_sem=s1_send.at[p], recv_sem=s1_recv.at[slot],
            device_id={"blk": xy_peer(p)})

    def s2(p, slot):
        return pltpu.make_async_remote_copy(
            src_ref=tbuf.at[0], dst_ref=s2buf.at[slot], send_sem=s2_send.at[p], recv_sem=s2_recv.at[slot],
            device_id={"blk": at(my, p, mx)})

    def s3(p, c, slot):
        return pltpu.make_async_remote_copy(
            src_ref=tbuf.at[1], dst_ref=g_ref.at[aligned(slot * 8, 8)],
            send_sem=s3_send.at[c * 16 + p], recv_sem=s3_recv.at[slot], device_id={"blk": xy_peer(p), "grp": c})

    xy = [(mxy + k) % 16 for k in range(1, 16)]
    line = [(mz + k) % NZ for k in range(1, NZ)]
    for p in xy:
        s1(p, mxy).start()
    total = hbuf[aligned(mxy * 8, 8), :]
    for p in xy:
        s1(p, p).wait_recv()
        total = total + s1buf[p]
    tbuf[0] = total
    s2buf[mz] = total
    for p in line:
        s2(p, mz).start()
    for p in line:
        s2(p, p).wait_recv()
    total = s2buf[0]
    for k in range(1, NZ):
        total = total + s2buf[k]
    tbuf[1] = total
    mine = core * 16 + mxy
    g_ref[aligned(mine * 8, 8), :] = total
    for p in xy:
        s3(p, core, mine).start()
        s3(p, other, mine).start()
    s3(mxy, other, mine).start()
    for p in xy:
        s3(p, core, core * 16 + p).wait_recv()
        s3(p, other, other * 16 + p).wait_recv()
    s3(mxy, other, other * 16 + mxy).wait_recv()
    for p in xy:
        s1(p, p).wait_send()
        s3(p, core, mine).wait_send()
        s3(p, other, mine).wait_send()
    s3(mxy, other, mine).wait_send()
    for p in line:
        s2(p, p).wait_send()

    def sent(k, _):
        copy((me + k) % NB, me).wait_send()
        return 0

    lax.fori_loop(1, NB, sent, 0)


def gather_and_gram(field, weight, response, table):
    dma = pltpu.SemaphoreType.DMA
    vmem = pl.BlockSpec(memory_space=pltpu.VMEM)
    hbm = pl.BlockSpec(memory_space=pltpu.HBM)
    return pl.pallas_call(
        gather_kernel,
        out_shape=(
            jax.ShapeDtypeStruct((COLS, ROWS), jnp.bfloat16),
            jax.ShapeDtypeStruct((COLS, COLS), jnp.float32),
            jax.ShapeDtypeStruct((MONTHS, MONTHS), jnp.float32),
            jax.ShapeDtypeStruct((1, ROWS), jnp.float32),
        ),
        in_specs=[hbm, hbm, hbm, hbm],
        out_specs=(vmem, vmem, vmem, vmem),
        scratch_shapes=[
            pltpu.VMEM((1, BINS), jnp.float32),
            pltpu.VMEM((4, MONTHS, BINS), jnp.float32),
            pltpu.VMEM((NB, 2, ROWS), jnp.bfloat16),
            pltpu.VMEM((COLS, COLS), jnp.float32),
            pltpu.VMEM((3 * GROUP, COLS), jnp.float32),
            pltpu.VMEM((COLS // 2, COLS), jnp.float32),
            pltpu.VMEM((COLS // 2, COLS), jnp.float32),
            pltpu.VMEM((16, 8, COLS), jnp.float32),
            pltpu.VMEM((NZ, 8, COLS), jnp.float32),
            pltpu.VMEM((2, 8, COLS), jnp.float32),
            pltpu.SemaphoreType.REGULAR((2,)),
            dma((4,)), dma((NB,)), dma((NB,)), dma, dma,
            dma((16,)), dma((16,)), dma((NZ,)), dma((NZ,)), dma((32,)), dma((32,)),
        ],
        compiler_params=pltpu.CompilerParams(
            collective_id=0, has_side_effects=True, vmem_limit_bytes=16 * 1024 * 1024),
        name="gather_gram",
    )(field, weight, response, table)


def shards(field, response, area_weight):
    gathered, raw, filt, weight = gather_and_gram(
        *(pltpu.with_memory_space_constraint(x, pltpu.HBM) for x in (field, area_weight.reshape(1, ROWS), response.reshape(1, BINS), jnp.asarray(filter_tables()))))
    return solve(raw, filt, weight, gathered)


def solution(mesh):
    in_specs = (P("blk", "grp"), P(), P(("grp", "blk")))
    out_specs = (P(None, ("grp", "blk")), P())
    return jax.shard_map(shards, mesh=mesh, in_specs=in_specs, out_specs=out_specs, check_vma=False)
```

time: 755 us -> 96.9 us (0.13); the launches traced: 744 us -> 96.8 us
  waiting for transfers between devices: 528 us -> 0 us
  other arithmetic: 133 us -> 0 us
  Pallas kernels: 0 us -> 96.2 us
  matrix products: 33.7 us -> 0 us
  starting transfers between devices: 16.6 us -> 0 us
  between operations: 17.1 us -> 0.64 us
  local copies, waits for them, and re-layouts: 15.1 us -> 0 us
    psum x2 -> x0, waiting for transfers between devices: 499 us -> none  [global_gram(): return lax.psum(matrix, ('grp', 'blk'))]
    another operation x17 -> x0, other arithmetic: 109 us -> none  [the longest x4 39.8 us: solve_lower(): return lax.linalg.triangular_solve(matrix, rhs, left_side=True, lower=True)]
    pallas_call x0 -> x2, Pallas kernels: none -> 96.2 us  [the longest x1 83.7 us: gather_and_gram(): pl.pallas_call(gather_kernel, out_shape=(jax.ShapeDtypeStruct((COLS, ROWS...]
    all_to_all x1 -> x0, waiting for transfers between devices: 28.8 us -> none  [shards(): lax.all_to_all(field, 'blk', split_axis=1, concat_axis=0, tiled=True)]
    dot_general x5 -> x0, matrix products: 17.7 us -> none  [the longest x2 8.46 us: gram_of(): jnp.dot(column_row_pairs, column_row_pairs.T, precision=TOP_PRECISION, pr...]
    all_to_all x1 -> x0, starting transfers between devices: 16.3 us -> none  [shards(): lax.all_to_all(field, 'blk', split_axis=1, concat_axis=0, tiled=True)]
    another operation x10 -> x0, matrix products: 16 us -> none  [the longest x6 15 us: solve_lower(): return lax.linalg.triangular_solve(matrix, rhs, left_side=True, lower=True)]
    cos x1 -> x0, other arithmetic: 15.4 us -> none  [filter_matrix(): table = jnp.cos(2.0 * jnp.pi * phase.astype(jnp.float32) / months)]
  transfers between devices with their start and end apart: 3 -> 0, of which waited for: 3 -> 0; matrix products, arithmetic and copies ran while one was open for 3% -> 0% of each run, Pallas kernels for 0% -> 0%
where the time goes in v3:
time: 96.9 us; the launch traced here: 96.8 us
  Pallas kernels  96.2 us (99%)
    pallas_call x1, Pallas kernels, gather_and_gram(): pl.pallas_call(gather_kernel, out_shape=(jax.ShapeDtypeStruct((COLS, ROWS...  83.7 us
    pallas_call x1, Pallas kernels, solve(): pl.pallas_call(solve_kernel, out_shape=(jax.ShapeDtypeStruct((COLS, ROWS)...  12.4 us

profile of v3, /device:TPU:1, one launch (start us, length us, event | category | flops | bytes accessed | tf_op | source)
XLA Modules:
  0.0 96.8 jit_solution(7701816575638042632)
XLA Ops:
  0.6 83.7 %gather_gram.1 = (bf16[256,4096]{1,0:T(8,128)(2,1)S(1)}, f32[256,256]{1,0:T(8,128)S(1)}, f32[128,128]{1,0:T(8,128)S(1)}, f32[1,4096]{1,0:T(1,128)S(1)}) custom-call(bf16[2,524288]{1,0:T(2,128)(2,1)} %field_ref.1, f32[1,4096]{1,0:T(1,128)} %bitcast.2, f32[1,65]{1,0:T(1,128)} %bitcast.3, f32[4,128,65]{2,1,0:T(8,128)} %constant.2.clone.table_in), custom_call_target="tpu_custom_call" | custom-call | tf_op jit(solution)/shard_map/gather_gram/pallas_call | solution.py:362
  84.4 12.4 %solve.1 = (f32[256,4096]{1,0:T(8,128)}, f32[256,256]{1,0:T(8,128)}) custom-call(f32[256,256]{1,0:T(8,128)S(1)} %get-tuple-element.6.raw_ref, f32[128,128]{1,0:T(8,128)S(1)} %get-tuple-element.7.filt_ref, f32[1,4096]{1,0:T(1,128)S(1)} %get-tuple-element.8.weight_ref, bf16[256,4096]{1,0:T(8,128)(2,1)S(1)} %get-tuple-element.9.f_ref), custom_call_target="tpu_custom_call" | custom-call | tf_op jit(solution)/shard_map/solve/pallas_call | solution.py:169

commit v4 on v3

--- a/solution.py
+++ b/solution.py
@@ -125,42 +125,44 @@
     work[half:, 2 * half:3 * half] = zero
     work[half:, 3 * half:] = mix
 
-    def put(i, k):
+    def put(i, first, count):
         return pltpu.make_async_copy(
-            obuf.at[i, aligned(k * half, half)],
-            out_ref.at[aligned(k * half, half), aligned(i * OUT_CHUNK, OUT_CHUNK)], osem.at[k, i])
-
-    def project(i, k, terms, depth):
-        lanes = aligned(i * OUT_CHUNK, OUT_CHUNK)
-        f = f_ref[:depth, lanes]
-        dot = lambda t: jnp.dot(t, f, preferred_element_type=jnp.float32)
-        high, middle, low = terms
-        obuf[i, k * half:(k + 1) * half, :] = (dot(low) + dot(middle) + dot(high)) * weight_ref[:, lanes]
-        put(i, k).start()
+            obuf.at[i, pl.ds(first, count)], out_ref.at[pl.ds(first, count), pl.ds(i * OUT_CHUNK, OUT_CHUNK)],
+            osem.at[first // 64, i])
+
+    def stacked(first, count, depth):
+        return jnp.concatenate(split3(work[first:first + count, 2 * half:2 * half + depth]), axis=0)
+
+    def project(i, terms, first, count, depth):
+        lanes = pl.ds(i * OUT_CHUNK, OUT_CHUNK)
+        parts = jnp.dot(terms, f_ref[:depth, lanes], preferred_element_type=jnp.float32)
+        total = parts[2 * count:] + parts[count:2 * count] + parts[:count]
+        obuf[i, first:first + count, :] = total * weight_ref[:, lanes]
+        put(i, first, count).start()
 
     for b in range(8):
         eliminate(work, b)
-    upper = split3(work[:half, 2 * half:3 * half])
-    for b in range(8, 16):
+    terms = stacked(0, half, half)
+    for b in range(8, 12):
         eliminate(work, b)
-        project(b - 8, 0, upper, half)
-    lower = split3(work[half:, 2 * half:])
-
-    def step(i, _):
-        project(i, 1, lower, COLS)
-        return 0
-
-    lax.fori_loop(0, OUT_STEPS, step, 0)
+        for i in (2 * b - 16, 2 * b - 15):
+            project(i, terms, 0, half, half)
+    terms = stacked(half, 64, COLS)
+    for b in range(12, 16):
+        eliminate(work, b)
+        for i in (2 * b - 24, 2 * b - 23):
+            project(i, terms, half, 64, COLS)
+    terms = stacked(half + 64, 64, COLS)
+    for i in range(OUT_STEPS):
+        project(i, terms, half + 64, 64, COLS)
     r = lax.broadcasted_iota(jnp.int32, (COLS, COLS), 0)
     c = lax.broadcasted_iota(jnp.int32, (COLS, COLS), 1)
     r_ref[...] = jnp.where(r <= c, work[:, :COLS], 0.0)
 
-    def done(i, _):
-        put(i, 0).wait()
-        put(i, 1).wait()
-        return 0
-
-    lax.fori_loop(0, OUT_STEPS, done, 0)
+    for i in range(OUT_STEPS):
+        put(i, 0, half).wait()
+        put(i, half, 64).wait()
+        put(i, half + 64, 64).wait()
 
 
 def solve(raw, filt, weight, gathered):
@@ -174,7 +176,7 @@
         scratch_shapes=[
             pltpu.VMEM((COLS, 4 * MONTHS), jnp.float32),
             pltpu.VMEM((OUT_STEPS, COLS, OUT_CHUNK), jnp.float32),
-            pltpu.SemaphoreType.DMA((2, OUT_STEPS)),
+            pltpu.SemaphoreType.DMA((4, OUT_STEPS)),
         ],
         compiler_params=pltpu.CompilerParams(vmem_limit_bytes=16 * 1024 * 1024),
         name="solve",
@@ -260,7 +262,25 @@
     filt_ref[...] = (
         dot_t(table_ref[2] * gain, table_ref[0], TOP) + dot_t(table_ref[3] * gain, table_ref[1], TOP))
 
-    def window(t, _):
+    share = GROUP // 2
+    owner_group = (my + 1) % NY
+
+    def pair(t, group):
+        return pltpu.make_async_remote_copy(
+            src_ref=gacc.at[aligned(group * GROUP + other * share, share)], dst_ref=pbuf.at[t],
+            send_sem=p_send.at[t], recv_sem=p_recv.at[t], device_id={"grp": other})
+
+    def s1(t, i, group, slot):
+        return pltpu.make_async_remote_copy(
+            src_ref=hbuf.at[t, aligned(i * 8, 8)], dst_ref=s1buf.at[slot], send_sem=s1_send.at[t * NX + i],
+            recv_sem=s1_recv.at[slot], device_id={"blk": at(group + NY - 1, mz, i)})
+
+    def s1_from(p):
+        return pltpu.make_async_remote_copy(
+            src_ref=hbuf.at[0, aligned(0, 8)], dst_ref=s1buf.at[p], send_sem=s1_send.at[0],
+            recv_sem=s1_recv.at[p], device_id={"blk": xy_peer(p)})
+
+    def window(t):
         group = (my + NY - t) % NY
 
         def arrive(i, _):
@@ -285,40 +305,48 @@
         total = terms[2 * GROUP:, :] + terms[GROUP:2 * GROUP, :] + terms[:GROUP, :]
         column = lax.broadcasted_iota(jnp.int32, (GROUP, COLS), 1)
         gacc[rows, :] = jnp.where(column // GROUP == group, 0.5 * total, total)
-        return 0
-
-    lax.fori_loop(0, NY, window, 0)
-
-    half = COLS // 2
-    pair = pltpu.make_async_remote_copy(
-        src_ref=gacc.at[aligned(other * half, half)], dst_ref=pbuf, send_sem=p_send, recv_sem=p_recv,
-        device_id={"grp": other})
-    pair.start()
-    pair.wait()
-    hbuf[...] = gacc[aligned(core * half, half), :] + pbuf[...]
-
-    def s1(p, slot):
-        return pltpu.make_async_remote_copy(
-            src_ref=hbuf.at[aligned(p * 8, 8)], dst_ref=s1buf.at[slot], send_sem=s1_send.at[p], recv_sem=s1_recv.at[slot],
-            device_id={"blk": xy_peer(p)})
+        pair(t, group).start()
+        pair(t, group).wait_recv()
+        hbuf[t] = gacc[aligned(group * GROUP + core * share, share), :] + pbuf[t]
+        return group
+
+    def early(t, _):
+        group = window(t)
+        for i in range(NX):
+            s1(t, i, group, mxy).start()
+        return 0
+
+    lax.fori_loop(0, NY - 1, early, 0)
+    window(NY - 1)
+    row = [(mx + k) % NX for k in range(1, NX)]
+    for i in row:
+        s1(NY - 1, i, owner_group, mxy).start()
 
     def s2(p, slot):
         return pltpu.make_async_remote_copy(
             src_ref=tbuf.at[0], dst_ref=s2buf.at[slot], send_sem=s2_send.at[p], recv_sem=s2_recv.at[slot],
             device_id={"blk": at(my, p, mx)})
 
-    def s3(p, c, slot):
-        return pltpu.make_async_remote_copy(
-            src_ref=tbuf.at[1], dst_ref=g_ref.at[aligned(slot * 8, 8)],
-            send_sem=s3_send.at[c * 16 + p], recv_sem=s3_recv.at[slot], device_id={"blk": xy_peer(p), "grp": c})
+    def piece(p, c):
+        y, x = p // NX, p % NX
+        return aligned(((y + 1) % NY) * GROUP + c * share + x * 8, 8)
+
+    def s3(p, c, q, d):
+        return pltpu.make_async_remote_copy(
+            src_ref=tbuf.at[1], dst_ref=g_ref.at[piece(q, d)],
+            send_sem=s3_send.at[c * 16 + p], recv_sem=s3_recv.at[d * 16 + q], device_id={"blk": xy_peer(p), "grp": c})
 
     xy = [(mxy + k) % 16 for k in range(1, 16)]
     line = [(mz + k) % NZ for k in range(1, NZ)]
-    for p in xy:
-        s1(p, mxy).start()
-    total = hbuf[aligned(mxy * 8, 8), :]
-    for p in xy:
-        s1(p, p).wait_recv()
+    total = hbuf[NY - 1, aligned(mx * 8, 8), :]
+    for k in range(1, NY):
+        for j in range(NX):
+            p = (my + k) % NY * NX + j
+            s1_from(p).wait_recv()
+            total = total + s1buf[p]
+    for i in row:
+        p = my * NX + i
+        s1_from(p).wait_recv()
         total = total + s1buf[p]
     tbuf[0] = total
     s2buf[mz] = total
@@ -330,23 +358,33 @@
     for k in range(1, NZ):
         total = total + s2buf[k]
     tbuf[1] = total
-    mine = core * 16 + mxy
-    g_ref[aligned(mine * 8, 8), :] = total
+    g_ref[piece(mxy, core), :] = total
     for p in xy:
-        s3(p, core, mine).start()
-        s3(p, other, mine).start()
-    s3(mxy, other, mine).start()
+        s3(p, core, mxy, core).start()
+        s3(p, other, mxy, core).start()
+    s3(mxy, other, mxy, core).start()
     for p in xy:
-        s3(p, core, core * 16 + p).wait_recv()
-        s3(p, other, other * 16 + p).wait_recv()
-    s3(mxy, other, other * 16 + mxy).wait_recv()
+        s3(p, core, p, core).wait_recv()
+        s3(p, other, p, other).wait_recv()
+    s3(mxy, other, mxy, other).wait_recv()
     for p in xy:
-        s1(p, p).wait_send()
-        s3(p, core, mine).wait_send()
-        s3(p, other, mine).wait_send()
-    s3(mxy, other, mine).wait_send()
+        s3(p, core, mxy, core).wait_send()
+        s3(p, other, mxy, core).wait_send()
+    s3(mxy, other, mxy, core).wait_send()
     for p in line:
         s2(p, p).wait_send()
+
+    def shared(t, _):
+        group = (my + NY - t) % NY
+        pair(t, group).wait_send()
+        for i in range(NX):
+            s1(t, i, group, mxy).wait_send()
+        return 0
+
+    lax.fori_loop(0, NY - 1, shared, 0)
+    pair(NY - 1, owner_group).wait_send()
+    for i in row:
+        s1(NY - 1, i, owner_group, mxy).wait_send()
 
     def sent(k, _):
         copy((me + k) % NB, me).wait_send()
@@ -375,13 +413,13 @@
             pltpu.VMEM((NB, 2, ROWS), jnp.bfloat16),
             pltpu.VMEM((COLS, COLS), jnp.float32),
             pltpu.VMEM((3 * GROUP, COLS), jnp.float32),
-            pltpu.VMEM((COLS // 2, COLS), jnp.float32),
-            pltpu.VMEM((COLS // 2, COLS), jnp.float32),
+            pltpu.VMEM((NY, GROUP // 2, COLS), jnp.float32),
+            pltpu.VMEM((NY, GROUP // 2, COLS), jnp.float32),
             pltpu.VMEM((16, 8, COLS), jnp.float32),
             pltpu.VMEM((NZ, 8, COLS), jnp.float32),
             pltpu.VMEM((2, 8, COLS), jnp.float32),
             pltpu.SemaphoreType.REGULAR((2,)),
-            dma((4,)), dma((NB,)), dma((NB,)), dma, dma,
+            dma((4,)), dma((NB,)), dma((NB,)), dma((NY,)), dma((NY,)),
             dma((16,)), dma((16,)), dma((NZ,)), dma((NZ,)), dma((32,)), dma((32,)),
         ],
         compiler_params=pltpu.CompilerParams(

time: 96.9 us -> 93.4 us (0.964)
  Pallas kernels: 96.2 us -> 92.7 us
    pallas_call x1, Pallas kernels: 83.7 us -> 81.9 us  [gather_and_gram(): pl.pallas_call(gather_kernel, out_shape=(jax.ShapeDtypeStruct((COLS, ROWS...]
    pallas_call x1, Pallas kernels: 12.4 us -> 10.8 us  [solve(): pl.pallas_call(solve_kernel, out_shape=(jax.ShapeDtypeStruct((COLS, ROWS)...]
where the time goes in v4:
time: 93.4 us; the launch traced here: 93.3 us
  Pallas kernels  92.7 us (99%)
    pallas_call x1, Pallas kernels, gather_and_gram(): pl.pallas_call(gather_kernel, out_shape=(jax.ShapeDtypeStruct((COLS, ROWS...  81.9 us
    pallas_call x1, Pallas kernels, solve(): pl.pallas_call(solve_kernel, out_shape=(jax.ShapeDtypeStruct((COLS, ROWS)...  10.8 us

profile of v4, /device:TPU:1, one launch (start us, length us, event | category | flops | bytes accessed | tf_op | source)
XLA Modules:
  0.0 93.3 jit_solution(16914499320379195427)
XLA Ops:
  0.6 81.9 %gather_gram.1 = (bf16[256,4096]{1,0:T(8,128)(2,1)S(1)}, f32[256,256]{1,0:T(8,128)S(1)}, f32[128,128]{1,0:T(8,128)S(1)}, f32[1,4096]{1,0:T(1,128)S(1)}) custom-call(bf16[2,524288]{1,0:T(2,128)(2,1)} %field_ref.1, f32[1,4096]{1,0:T(1,128)} %bitcast.2, f32[1,65]{1,0:T(1,128)} %bitcast.3, f32[4,128,65]{2,1,0:T(8,128)} %constant.2.clone.table_in), custom_call_target="tpu_custom_call" | custom-call | tf_op jit(solution)/shard_map/gather_gram/pallas_call | solution.py:400
  82.5 10.8 %solve.1 = (f32[256,4096]{1,0:T(8,128)}, f32[256,256]{1,0:T(8,128)}) custom-call(f32[256,256]{1,0:T(8,128)S(1)} %get-tuple-element.6.raw_ref, f32[128,128]{1,0:T(8,128)S(1)} %get-tuple-element.7.filt_ref, f32[1,4096]{1,0:T(1,128)S(1)} %get-tuple-element.8.weight_ref, bf16[256,4096]{1,0:T(8,128)(2,1)S(1)} %get-tuple-element.9.f_ref), custom_call_target="tpu_custom_call" | custom-call | tf_op jit(solution)/shard_map/solve/pallas_call | solution.py:171

commit v5 on v4

--- a/solution.py
+++ b/solution.py
@@ -29,7 +29,8 @@
     coef = np.where(edge, 1.0, 2.0) / MONTHS
     angle = 2.0 * np.pi * ((np.arange(MONTHS)[:, None] * freq[None, :]) % MONTHS) / MONTHS
     cos, sin = np.cos(angle), np.sin(angle)
-    return np.stack([cos, sin, cos * coef, sin * coef]).astype(np.float32)
+    order = np.arange(MONTHS).reshape(-1, NZ, NX, 2).transpose(0, 2, 1, 3).reshape(-1)
+    return np.stack([cos[order], sin[order], cos * coef, sin * coef]).astype(np.float32)
 
 
 def split3(value):
@@ -185,7 +186,7 @@
 
 def gather_kernel(
     field_ref, weight_in, response_in, table_in, f_ref, g_ref, filt_ref, weight_ref,
-    response_ref, table_ref, fbuf, gacc, terms, pbuf, hbuf, s1buf, s2buf, tbuf,
+    response_ref, table_ref, fbuf, gacc, pieces, pbuf, hbuf, s1buf, s2buf, tbuf,
     phase, own_sem, a_send, a_recv, p_send, p_recv, s1_send, s1_recv, s2_send, s2_recv, s3_send, s3_recv,
 ):
     core = lax.axis_index("grp")
@@ -205,10 +206,14 @@
     def signal(sem, **where):
         pl.semaphore_signal(sem, inc=1, device_id=where)
 
+    def slot_of(p):
+        return p // PLANE * PLANE + p % NX * NZ + p // NX % NZ
+
     def cut(p):
         return field_ref.at[:, aligned(p * ROWS, ROWS)]
 
-    def copy(p, slot):
+    def copy(p, source):
+        slot = slot_of(source)
         return pltpu.make_async_remote_copy(
             src_ref=cut(p), dst_ref=fbuf.at[slot], send_sem=a_send.at[p], recv_sem=a_recv.at[slot],
             device_id={"blk": p})
@@ -231,7 +236,7 @@
 
     lax.fori_loop(1, NZ, send_line, 0)
     local = [
-        pltpu.make_async_copy(cut(me), fbuf.at[me], own_sem.at[0]),
+        pltpu.make_async_copy(cut(me), fbuf.at[slot_of(me)], own_sem.at[0]),
         pltpu.make_async_copy(weight_in, weight_ref, own_sem.at[1]),
         pltpu.make_async_copy(response_in, response_ref, own_sem.at[2]),
         pltpu.make_async_copy(table_in, table_ref, own_sem.at[3]),
@@ -283,25 +288,32 @@
     def window(t):
         group = (my + NY - t) % NY
 
-        def arrive(i, _):
-            p = group * PLANE + (mz * NX + mx + i) % PLANE
-            copy(p, p).wait_recv()
+        def batch(q, _):
+            x = (mx + NX - q) % NX
+
+            def arrive(i, _):
+                p = at(group, mz + i, x)
+                copy(p, p).wait_recv()
+                return 0
+
+            lax.fori_loop(jnp.where(t + q == 0, 1, 0), NZ, arrive, 0)
+            start = x * BLOCK
+
+            def unpack(c, _):
+                lanes = aligned(c * CHUNK, CHUNK)
+                block = fbuf[aligned(group * PLANE + x * NZ, NZ), :, lanes].reshape(BLOCK, CHUNK)
+                f_ref[aligned(group * GROUP + start, BLOCK), lanes] = block
+                w = weight_ref[:, lanes]
+                for k, part in enumerate(split3(block.astype(jnp.float32) * (w * w))):
+                    pieces[aligned(k * GROUP + start, BLOCK), lanes] = part
+                return 0
+
+            lax.fori_loop(0, ROWS // CHUNK, unpack, 0)
             return 0
 
-        lax.fori_loop(jnp.where(t == 0, 1, 0), PLANE, arrive, 0)
+        lax.fori_loop(0, NX, batch, 0)
         rows = aligned(group * GROUP, GROUP)
-        terms[...] = jnp.zeros_like(terms)
-
-        def gram(c, _):
-            lanes = aligned(c * CHUNK, CHUNK)
-            block = fbuf[aligned(group * PLANE, PLANE), :, lanes].reshape(GROUP, CHUNK)
-            f_ref[rows, lanes] = block
-            w = weight_ref[:, lanes]
-            pieces = jnp.concatenate(split3(block.astype(jnp.float32) * (w * w)), axis=0)
-            terms[...] += dot_t(pieces, f_ref[:, lanes])
-            return 0
-
-        lax.fori_loop(0, ROWS // CHUNK, gram, 0)
+        terms = dot_t(pieces[...], f_ref[...])
         total = terms[2 * GROUP:, :] + terms[GROUP:2 * GROUP, :] + terms[:GROUP, :]
         column = lax.broadcasted_iota(jnp.int32, (GROUP, COLS), 1)
         gacc[rows, :] = jnp.where(column // GROUP == group, 0.5 * total, total)
@@ -412,7 +424,7 @@
             pltpu.VMEM((4, MONTHS, BINS), jnp.float32),
             pltpu.VMEM((NB, 2, ROWS), jnp.bfloat16),
             pltpu.VMEM((COLS, COLS), jnp.float32),
-            pltpu.VMEM((3 * GROUP, COLS), jnp.float32),
+            pltpu.VMEM((3 * GROUP, ROWS), jnp.bfloat16),
             pltpu.VMEM((NY, GROUP // 2, COLS), jnp.float32),
             pltpu.VMEM((NY, GROUP // 2, COLS), jnp.float32),
             pltpu.VMEM((16, 8, COLS), jnp.float32),

time: 93.4 us -> 92.8 us (level)
  no operation moved by 1% of the time
where the time goes in v5:
time: 92.8 us; the launch traced here: 92.7 us
  Pallas kernels  92.1 us (99%)
    pallas_call x1, Pallas kernels, gather_and_gram(): pl.pallas_call(gather_kernel, out_shape=(jax.ShapeDtypeStruct((COLS, ROWS...  81.2 us
    pallas_call x1, Pallas kernels, solve(): pl.pallas_call(solve_kernel, out_shape=(jax.ShapeDtypeStruct((COLS, ROWS)...  10.8 us

profile of v5, /device:TPU:1, one launch (start us, length us, event | category | flops | bytes accessed | tf_op | source)
XLA Modules:
  0.0 92.7 jit_solution(9351208917179388956)
XLA Ops:
  0.6 81.2 %gather_gram.1 = (bf16[256,4096]{1,0:T(8,128)(2,1)S(1)}, f32[256,256]{1,0:T(8,128)S(1)}, f32[128,128]{1,0:T(8,128)S(1)}, f32[1,4096]{1,0:T(1,128)S(1)}) custom-call(bf16[2,524288]{1,0:T(2,128)(2,1)} %field_ref.1, f32[1,4096]{1,0:T(1,128)} %bitcast.2, f32[1,65]{1,0:T(1,128)} %bitcast.3, f32[4,128,65]{2,1,0:T(8,128)} %constant.2.clone.table_in), custom_call_target="tpu_custom_call" | custom-call | tf_op jit(solution)/shard_map/gather_gram/pallas_call | solution.py:412
  81.9 10.8 %solve.1 = (f32[256,4096]{1,0:T(8,128)}, f32[256,256]{1,0:T(8,128)}) custom-call(f32[256,256]{1,0:T(8,128)S(1)} %get-tuple-element.6.raw_ref, f32[128,128]{1,0:T(8,128)S(1)} %get-tuple-element.7.filt_ref, f32[1,4096]{1,0:T(1,128)S(1)} %get-tuple-element.8.weight_ref, bf16[256,4096]{1,0:T(8,128)(2,1)S(1)} %get-tuple-element.9.f_ref), custom_call_target="tpu_custom_call" | custom-call | tf_op jit(solution)/shard_map/solve/pallas_call | solution.py:172

commit v6 on v5

--- a/solution.py
+++ b/solution.py
@@ -21,6 +21,7 @@
 WIDE = 384
 OUT_CHUNK = 512
 OUT_STEPS = ROWS // OUT_CHUNK
+FAR_FIRST = sorted(((y, x) for y in range(NY) for x in range(NX) if y or x), key=lambda s: -min(s[0], NY - s[0]) - min(s[1], NX - s[1]))
 
 
 def filter_tables():
@@ -65,14 +66,15 @@
     for j in range(BLOCK):
         if j < 8:
             d = lax.rsqrt(row_of(ct[j], j))
-            lt = jnp.where(sub > j, ct[j] * d, 0.0)
+            lt = ct[j] * d
             lb = cb[j] * d
             for k in range(j + 1, 8):
-                f = row_of(lt, k)
+                f = row_of(ct[j], k) * d if k == j + 1 else row_of(lt, k)
                 ct[k] = ct[k] - lt * f
                 cb[k] = cb[k] - lb * f
             for k in range(8, 16):
                 cb[k] = cb[k] - lb * row_of(lb, k - 8)
+            lt = jnp.where(sub > j, lt, 0.0)
             for t in range(3):
                 u = row_of(top[t], j) * d
                 bot[t] = bot[t] - lb * u
@@ -80,9 +82,10 @@
         else:
             i = j - 8
             d = lax.rsqrt(row_of(cb[j], i))
-            lb = jnp.where(sub > i, cb[j] * d, 0.0)
+            lb = cb[j] * d
             for k in range(j + 1, 16):
-                cb[k] = cb[k] - lb * row_of(lb, k - 8)
+                cb[k] = cb[k] - lb * (row_of(cb[j], k - 8) * d if k == j + 1 else row_of(lb, k - 8))
+            lb = jnp.where(sub > i, lb, 0.0)
             for t in range(3):
                 u = row_of(bot[t], i) * d
                 bot[t] = jnp.where(sub == i, u, bot[t] - lb * u)
@@ -100,16 +103,17 @@
     cut = lambda x: x[:, left:left + width]
     a = jnp.concatenate([cut(h), cut(h), cut(m), cut(h), cut(l), cut(m)], axis=0)
     c = jnp.concatenate([h, m, h, l, h, m], axis=0)
-    prod = lax.dot_general(a, c, (((0,), (0,)), ((), ())), preferred_element_type=jnp.float32)
-    work[nxt:COLS, base:base + WIDE] = work[nxt:COLS, base:base + WIDE] - prod[nxt - first:, :]
+    a = a.T
+    skip = nxt - first
+    for start, stop in ((nxt, nxt + BLOCK), (nxt + BLOCK, COLS)):
+        if start < stop:
+            prod = jnp.dot(a[start - first:stop - first], c, preferred_element_type=jnp.float32)
+            work[start:stop, base:base + WIDE] = work[start:stop, base:base + WIDE] - prod
 
 
 def solve_kernel(raw_ref, filt_ref, weight_ref, f_ref, out_ref, r_ref, work, obuf, osem):
     mix = filt_ref[...]
     half = MONTHS
-
-    def side(block):
-        return jnp.dot(mix, dot_t(block, mix, TOP), precision=TOP, preferred_element_type=jnp.float32)
 
     def fold(i, j):
         first = raw_ref[i * half:(i + 1) * half, j * half:(j + 1) * half]
@@ -117,9 +121,13 @@
         return (first + second.T) * (1.0 / POINTS)
 
     zero = jnp.zeros((half, half), jnp.float32)
-    work[:half, :half] = side(fold(0, 0))
-    work[:half, half:2 * half] = side(fold(0, 1))
-    work[half:, half:2 * half] = side(fold(1, 1))
+    sides = [dot_t(fold(0, 0), mix, TOP), dot_t(fold(0, 1), mix, TOP)]
+    for rows in (slice(0, BLOCK), slice(BLOCK, half)):
+        for k, right in enumerate(sides):
+            work[rows, k * half:(k + 1) * half] = jnp.dot(
+                mix[rows], right, precision=TOP, preferred_element_type=jnp.float32)
+    last = dot_t(fold(1, 1), mix, TOP)
+    work[half:, half:2 * half] = jnp.dot(mix, last, precision=TOP, preferred_element_type=jnp.float32)
     work[half:, :half] = zero
     work[:half, 2 * half:3 * half] = mix
     work[:half, 3 * half:] = zero
@@ -248,14 +256,14 @@
         signal(phase.at[1], blk=at(my + k, mz, mx))
 
     def send_plane(i, _):
-        copy(at(my, mz + i % NZ, mx + 1 + i // NZ), me).start()
+        copy(at(my, mz + 4 + (i % NZ) * 3, mx + 1 + i // NZ), me).start()
         return 0
 
     lax.fori_loop(0, PLANE - NZ, send_plane, 0)
     pl.semaphore_wait(phase.at[1], NY - 1)
 
     def send_rest(i, _):
-        copy(at(my + 1 + i // PLANE, mz + i % NZ, mx + (i // NZ) % NX), me).start()
+        copy(at(my + 1 + i // PLANE, mz + 4 + (i % NZ) * 3, mx + (i // NZ) % NX), me).start()
         return 0
 
     lax.fori_loop(0, NB - PLANE, send_rest, 0)
@@ -348,8 +356,8 @@
             src_ref=tbuf.at[1], dst_ref=g_ref.at[piece(q, d)],
             send_sem=s3_send.at[c * 16 + p], recv_sem=s3_recv.at[d * 16 + q], device_id={"blk": xy_peer(p), "grp": c})
 
-    xy = [(mxy + k) % 16 for k in range(1, 16)]
-    line = [(mz + k) % NZ for k in range(1, NZ)]
+    xy = [(my + y) % NY * NX + (mx + x) % NX for y, x in FAR_FIRST]
+    line = [(mz + k) % NZ for k in (4, 3, 5, 2, 6, 1, 7)]
     total = hbuf[NY - 1, aligned(mx * 8, 8), :]
     for k in range(1, NY):
         for j in range(NX):

time: 92.8 us -> 90.6 us (0.976)
  Pallas kernels: 92.1 us -> 89.9 us
    pallas_call x1, Pallas kernels: 81.2 us -> 79.8 us  [gather_and_gram(): pl.pallas_call(gather_kernel, out_shape=(jax.ShapeDtypeStruct((COLS, ROWS...]
where the time goes in v6:
time: 90.6 us; the launch traced here: 90.5 us
  Pallas kernels  89.9 us (99%)
    pallas_call x1, Pallas kernels, gather_and_gram(): pl.pallas_call(gather_kernel, out_shape=(jax.ShapeDtypeStruct((COLS, ROWS...  79.8 us
    pallas_call x1, Pallas kernels, solve(): pl.pallas_call(solve_kernel, out_shape=(jax.ShapeDtypeStruct((COLS, ROWS)...  10.1 us

profile of v6, /device:TPU:1, one launch (start us, length us, event | category | flops | bytes accessed | tf_op | source)
XLA Modules:
  0.0 90.5 jit_solution(13221764584607932922)
XLA Ops:
  0.6 79.8 %gather_gram.1 = (bf16[256,4096]{1,0:T(8,128)(2,1)S(1)}, f32[256,256]{1,0:T(8,128)S(1)}, f32[128,128]{1,0:T(8,128)S(1)}, f32[1,4096]{1,0:T(1,128)S(1)}) custom-call(bf16[2,524288]{1,0:T(2,128)(2,1)} %field_ref.1, f32[1,4096]{1,0:T(1,128)} %bitcast.2, f32[1,65]{1,0:T(1,128)} %bitcast.3, f32[4,128,65]{2,1,0:T(8,128)} %constant.2.clone.table_in), custom_call_target="tpu_custom_call" | custom-call | tf_op jit(solution)/shard_map/gather_gram/pallas_call | solution.py:420
  80.4 10.1 %solve.1 = (f32[256,4096]{1,0:T(8,128)}, f32[256,256]{1,0:T(8,128)}) custom-call(f32[256,256]{1,0:T(8,128)S(1)} %get-tuple-element.6.raw_ref, f32[128,128]{1,0:T(8,128)S(1)} %get-tuple-element.7.filt_ref, f32[1,4096]{1,0:T(1,128)S(1)} %get-tuple-element.8.weight_ref, bf16[256,4096]{1,0:T(8,128)(2,1)S(1)} %get-tuple-element.9.f_ref), custom_call_target="tpu_custom_call" | custom-call | tf_op jit(solution)/shard_map/solve/pallas_call | solution.py:180

commit v7 on v6

--- a/solution.py
+++ b/solution.py
@@ -111,7 +111,7 @@
             work[start:stop, base:base + WIDE] = work[start:stop, base:base + WIDE] - prod
 
 
-def solve_kernel(raw_ref, filt_ref, weight_ref, f_ref, out_ref, r_ref, work, obuf, osem):
+def solve_kernel(raw_ref, filt_ref, weight_ref, f_ref, out_ref, r_ref, work, obuf, rbuf, osem, rsem):
     mix = filt_ref[...]
     half = MONTHS
 
@@ -161,13 +161,15 @@
         eliminate(work, b)
         for i in (2 * b - 24, 2 * b - 23):
             project(i, terms, half, 64, COLS)
+    r = lax.broadcasted_iota(jnp.int32, (COLS, COLS), 0)
+    c = lax.broadcasted_iota(jnp.int32, (COLS, COLS), 1)
+    rbuf[...] = jnp.where(r <= c, work[:, :COLS], 0.0)
+    triangle = pltpu.make_async_copy(rbuf, r_ref, rsem)
+    triangle.start()
     terms = stacked(half + 64, 64, COLS)
     for i in range(OUT_STEPS):
         project(i, terms, half + 64, 64, COLS)
-    r = lax.broadcasted_iota(jnp.int32, (COLS, COLS), 0)
-    c = lax.broadcasted_iota(jnp.int32, (COLS, COLS), 1)
-    r_ref[...] = jnp.where(r <= c, work[:, :COLS], 0.0)
-
+    triangle.wait()
     for i in range(OUT_STEPS):
         put(i, 0, half).wait()
         put(i, half, 64).wait()
@@ -181,11 +183,13 @@
         solve_kernel,
         out_shape=(jax.ShapeDtypeStruct((COLS, ROWS), jnp.float32), jax.ShapeDtypeStruct((COLS, COLS), jnp.float32)),
         in_specs=[vmem, vmem, vmem, vmem],
-        out_specs=(hbm, vmem),
+        out_specs=(hbm, hbm),
         scratch_shapes=[
             pltpu.VMEM((COLS, 4 * MONTHS), jnp.float32),
             pltpu.VMEM((OUT_STEPS, COLS, OUT_CHUNK), jnp.float32),
+            pltpu.VMEM((COLS, COLS), jnp.float32),
             pltpu.SemaphoreType.DMA((4, OUT_STEPS)),
+            pltpu.SemaphoreType.DMA,
         ],
         compiler_params=pltpu.CompilerParams(vmem_limit_bytes=16 * 1024 * 1024),
         name="solve",
@@ -238,6 +242,9 @@
     for k in range(1, NX):
         signal(phase.at[0], blk=at(my, mz, mx + k))
 
+    def far(i):
+        return 4 + (i // 2) * (1 - i % 2) - ((i + 1) // 2) * (i % 2) + NZ
+
     def send_line(i, _):
         copy(at(my, mz + i, mx), me).start()
         return 0
@@ -256,14 +263,14 @@
         signal(phase.at[1], blk=at(my + k, mz, mx))
 
     def send_plane(i, _):
-        copy(at(my, mz + 4 + (i % NZ) * 3, mx + 1 + i // NZ), me).start()
+        copy(at(my, mz + far(i % NZ), mx + 1 + i // NZ), me).start()
         return 0
 
     lax.fori_loop(0, PLANE - NZ, send_plane, 0)
     pl.semaphore_wait(phase.at[1], NY - 1)
 
     def send_rest(i, _):
-        copy(at(my + 1 + i // PLANE, mz + 4 + (i % NZ) * 3, mx + (i // NZ) % NX), me).start()
+        copy(at(my + 1 + i // PLANE, mz + far(i % NZ), mx + (i // NZ) % NX), me).start()
         return 0
 
     lax.fori_loop(0, NB - PLANE, send_rest, 0)
@@ -372,6 +379,25 @@
     s2buf[mz] = total
     for p in line:
         s2(p, mz).start()
+
+    def sent(k, _):
+        copy((me + k) % NB, me).wait_send()
+        return 0
+
+    lax.fori_loop(1, NB, sent, 0)
+
+    def shared(t, _):
+        group = (my + NY - t) % NY
+        pair(t, group).wait_send()
+        for i in range(NX):
+            s1(t, i, group, mxy).wait_send()
+        return 0
+
+    lax.fori_loop(0, NY - 1, shared, 0)
+    pair(NY - 1, owner_group).wait_send()
+    for i in row:
+        s1(NY - 1, i, owner_group, mxy).wait_send()
+
     for p in line:
         s2(p, p).wait_recv()
     total = s2buf[0]
@@ -393,24 +419,6 @@
     s3(mxy, other, mxy, core).wait_send()
     for p in line:
         s2(p, p).wait_send()
-
-    def shared(t, _):
-        group = (my + NY - t) % NY
-        pair(t, group).wait_send()
-        for i in range(NX):
-            s1(t, i, group, mxy).wait_send()
-        return 0
-
-    lax.fori_loop(0, NY - 1, shared, 0)
-    pair(NY - 1, owner_group).wait_send()
-    for i in row:
-        s1(NY - 1, i, owner_group, mxy).wait_send()
-
-    def sent(k, _):
-        copy((me + k) % NB, me).wait_send()
-        return 0
-
-    lax.fori_loop(1, NB, sent, 0)
 
 
 def gather_and_gram(field, weight, response, table):

time: 90.6 us -> 87.6 us (0.967)
  Pallas kernels: 89.9 us -> 86.9 us
    pallas_call x1, Pallas kernels: 79.8 us -> 77.5 us  [gather_and_gram(): pl.pallas_call(gather_kernel, out_shape=(jax.ShapeDtypeStruct((COLS, ROWS...]
where the time goes in v7:
time: 87.6 us; the launch traced here: 87.5 us
  Pallas kernels  86.9 us (99%)
    pallas_call x1, Pallas kernels, gather_and_gram(): pl.pallas_call(gather_kernel, out_shape=(jax.ShapeDtypeStruct((COLS, ROWS...  77.5 us
    pallas_call x1, Pallas kernels, solve(): pl.pallas_call(solve_kernel, out_shape=(jax.ShapeDtypeStruct((COLS, ROWS)...  9.43 us

profile of v7, /device:TPU:1, one launch (start us, length us, event | category | flops | bytes accessed | tf_op | source)
XLA Modules:
  0.0 87.5 jit_solution(6385556959055344091)
XLA Ops:
  0.6 77.5 %gather_gram.1 = (bf16[256,4096]{1,0:T(8,128)(2,1)S(1)}, f32[256,256]{1,0:T(8,128)S(1)}, f32[128,128]{1,0:T(8,128)S(1)}, f32[1,4096]{1,0:T(1,128)S(1)}) custom-call(bf16[2,524288]{1,0:T(2,128)(2,1)} %field_ref.1, f32[1,4096]{1,0:T(1,128)} %bitcast.2, f32[1,65]{1,0:T(1,128)} %bitcast.3, f32[4,128,65]{2,1,0:T(8,128)} %constant.2.clone.table_in), custom_call_target="tpu_custom_call" | custom-call | tf_op jit(solution)/shard_map/gather_gram/pallas_call | solution.py:428
  78.1 9.4 %solve.1 = (f32[256,4096]{1,0:T(8,128)}, f32[256,256]{1,0:T(8,128)}) custom-call(f32[256,256]{1,0:T(8,128)S(1)} %get-tuple-element.6.raw_ref, f32[128,128]{1,0:T(8,128)S(1)} %get-tuple-element.7.filt_ref, f32[1,4096]{1,0:T(1,128)S(1)} %get-tuple-element.8.weight_ref, bf16[256,4096]{1,0:T(8,128)(2,1)S(1)} %get-tuple-element.9.f_ref), custom_call_target="tpu_custom_call" | custom-call | tf_op jit(solution)/shard_map/solve/pallas_call | solution.py:182

commit v8 on v7

--- a/solution.py
+++ b/solution.py
@@ -19,7 +19,7 @@
 CHUNK = 1024
 BLOCK = 16
 WIDE = 384
-OUT_CHUNK = 512
+OUT_CHUNK = 1024
 OUT_STEPS = ROWS // OUT_CHUNK
 FAR_FIRST = sorted(((y, x) for y in range(NY) for x in range(NX) if y or x), key=lambda s: -min(s[0], NY - s[0]) - min(s[1], NX - s[1]))
 
@@ -121,13 +121,17 @@
         return (first + second.T) * (1.0 / POINTS)
 
     zero = jnp.zeros((half, half), jnp.float32)
-    sides = [dot_t(fold(0, 0), mix, TOP), dot_t(fold(0, 1), mix, TOP)]
+    def six(value, left, axis):
+        h, m, l = split3(value)
+        return jnp.concatenate([h, h, m, h, l, m] if left else [h, m, h, l, h, m], axis=axis)
+
+    wide = six(mix, True, 1)
+    product = lambda rows, right: jnp.dot(rows, six(right, False, 0), preferred_element_type=jnp.float32)
+    sides = [dot_t(six(fold(0, k), False, 1), wide) for k in range(2)]
     for rows in (slice(0, BLOCK), slice(BLOCK, half)):
         for k, right in enumerate(sides):
-            work[rows, k * half:(k + 1) * half] = jnp.dot(
-                mix[rows], right, precision=TOP, preferred_element_type=jnp.float32)
-    last = dot_t(fold(1, 1), mix, TOP)
-    work[half:, half:2 * half] = jnp.dot(mix, last, precision=TOP, preferred_element_type=jnp.float32)
+            work[rows, k * half:(k + 1) * half] = product(wide[rows], right)
+    work[half:, half:2 * half] = product(wide, dot_t(six(fold(1, 1), False, 1), wide))
     work[half:, :half] = zero
     work[:half, 2 * half:3 * half] = mix
     work[:half, 3 * half:] = zero
@@ -154,12 +158,12 @@
     terms = stacked(0, half, half)
     for b in range(8, 12):
         eliminate(work, b)
-        for i in (2 * b - 16, 2 * b - 15):
+        for i in (b - 8,):
             project(i, terms, 0, half, half)
     terms = stacked(half, 64, COLS)
     for b in range(12, 16):
         eliminate(work, b)
-        for i in (2 * b - 24, 2 * b - 23):
+        for i in (b - 12,):
             project(i, terms, half, 64, COLS)
     r = lax.broadcasted_iota(jnp.int32, (COLS, COLS), 0)
     c = lax.broadcasted_iota(jnp.int32, (COLS, COLS), 1)
@@ -231,7 +235,7 @@
             device_id={"blk": p})
 
     barrier = pltpu.get_barrier_semaphore()
-    for k in range(1, NZ):
+    for k in (4, 3, 5, 2, 6, 1, 7):
         signal(barrier, blk=at(my, mz + k, mx))
     for k in range(1, NX):
         signal(barrier, blk=at(my, mz, mx + k))
@@ -246,10 +250,10 @@
         return 4 + (i // 2) * (1 - i % 2) - ((i + 1) // 2) * (i % 2) + NZ
 
     def send_line(i, _):
-        copy(at(my, mz + i, mx), me).start()
-        return 0
-
-    lax.fori_loop(1, NZ, send_line, 0)
+        copy(at(my, mz + far(i), mx), me).start()
+        return 0
+
+    lax.fori_loop(0, NZ - 1, send_line, 0)
     local = [
         pltpu.make_async_copy(cut(me), fbuf.at[slot_of(me)], own_sem.at[0]),
         pltpu.make_async_copy(weight_in, weight_ref, own_sem.at[1]),

time: 87.6 us -> 87 us (level)
  no operation moved by 1% of the time
where the time goes in v8:
time: 87 us; the launch traced here: 86.9 us
  Pallas kernels  86.2 us (99%)
    pallas_call x1, Pallas kernels, gather_and_gram(): pl.pallas_call(gather_kernel, out_shape=(jax.ShapeDtypeStruct((COLS, ROWS...  77.2 us
    pallas_call x1, Pallas kernels, solve(): pl.pallas_call(solve_kernel, out_shape=(jax.ShapeDtypeStruct((COLS, ROWS)...  9.05 us

profile of v8, /device:TPU:1, one launch (start us, length us, event | category | flops | bytes accessed | tf_op | source)
XLA Modules:
  0.0 86.9 jit_solution(7218267468865835122)
XLA Ops:
  0.6 77.2 %gather_gram.1 = (bf16[256,4096]{1,0:T(8,128)(2,1)S(1)}, f32[256,256]{1,0:T(8,128)S(1)}, f32[128,128]{1,0:T(8,128)S(1)}, f32[1,4096]{1,0:T(1,128)S(1)}) custom-call(bf16[2,524288]{1,0:T(2,128)(2,1)} %field_ref.1, f32[1,4096]{1,0:T(1,128)} %bitcast.2, f32[1,65]{1,0:T(1,128)} %bitcast.3, f32[4,128,65]{2,1,0:T(8,128)} %constant.2.clone.table_in), custom_call_target="tpu_custom_call" | custom-call | tf_op jit(solution)/shard_map/gather_gram/pallas_call | solution.py:432
  77.8 9.0 %solve.1 = (f32[256,4096]{1,0:T(8,128)}, f32[256,256]{1,0:T(8,128)}) custom-call(f32[256,256]{1,0:T(8,128)S(1)} %get-tuple-element.6.raw_ref, f32[128,128]{1,0:T(8,128)S(1)} %get-tuple-element.7.filt_ref, f32[1,4096]{1,0:T(1,128)S(1)} %get-tuple-element.8.weight_ref, bf16[256,4096]{1,0:T(8,128)(2,1)S(1)} %get-tuple-element.9.f_ref), custom_call_target="tpu_custom_call" | custom-call | tf_op jit(solution)/shard_map/solve/pallas_call | solution.py:186

commit v9 on v8

--- a/solution.py
+++ b/solution.py
@@ -16,7 +16,7 @@
 NB = NY * NZ * NX
 PLANE = NZ * NX
 GROUP = 2 * PLANE
-CHUNK = 1024
+CHUNK = 2048
 BLOCK = 16
 WIDE = 384
 OUT_CHUNK = 1024

time: 87 us -> 86.9 us (level)
  no operation moved by 1% of the time
where the time goes in v9:
time: 86.9 us
  Pallas kernels  86.2 us (99%)
    pallas_call x1, Pallas kernels, gather_and_gram(): pl.pallas_call(gather_kernel, out_shape=(jax.ShapeDtypeStruct((COLS, ROWS...  77.2 us
    pallas_call x1, Pallas kernels, solve(): pl.pallas_call(solve_kernel, out_shape=(jax.ShapeDtypeStruct((COLS, ROWS)...  9.05 us

profile of v9, /device:TPU:1, one launch (start us, length us, event | category | flops | bytes accessed | tf_op | source)
XLA Modules:
  0.0 86.9 jit_solution(4447789903648342425)
XLA Ops:
  0.6 77.2 %gather_gram.1 = (bf16[256,4096]{1,0:T(8,128)(2,1)S(1)}, f32[256,256]{1,0:T(8,128)S(1)}, f32[128,128]{1,0:T(8,128)S(1)}, f32[1,4096]{1,0:T(1,128)S(1)}) custom-call(bf16[2,524288]{1,0:T(2,128)(2,1)} %field_ref.1, f32[1,4096]{1,0:T(1,128)} %bitcast.2, f32[1,65]{1,0:T(1,128)} %bitcast.3, f32[4,128,65]{2,1,0:T(8,128)} %constant.2.clone.table_in), custom_call_target="tpu_custom_call" | custom-call | tf_op jit(solution)/shard_map/gather_gram/pallas_call | solution.py:432
  77.8 9.1 %solve.1 = (f32[256,4096]{1,0:T(8,128)}, f32[256,256]{1,0:T(8,128)}) custom-call(f32[256,256]{1,0:T(8,128)S(1)} %get-tuple-element.6.raw_ref, f32[128,128]{1,0:T(8,128)S(1)} %get-tuple-element.7.filt_ref, f32[1,4096]{1,0:T(1,128)S(1)} %get-tuple-element.8.weight_ref, bf16[256,4096]{1,0:T(8,128)(2,1)S(1)} %get-tuple-element.9.f_ref), custom_call_target="tpu_custom_call" | custom-call | tf_op jit(solution)/shard_map/solve/pallas_call | solution.py:186
